TPU v7x, 32 devices: a whole 2x2x4 slice. The times are simulated.
32 devices in a mesh: outer: 4 (over y, x), rep: 4 (over z), shard: 2 (over core).
Axes of the slice: x: 2, y: 2, z: 4, core: 2. Of those that a mesh axis runs over, the one named last changes fastest.
Arguments:
- deltas: bfloat16 [4, 4, 1024, 5120], P('outer', 'rep', 'shard'), may hold values from -1400 to 1400, as said below
- owners: int32 [2, 4, 1], P('shard'), may hold values from 0 to 3; in each aligned block of 4 rows (0 to 3, 4 to 7, ..., all dimensions but the last counted through in order) at most 2 rows name the same one
- master: float32 [4, 2, 2, 128, 5120], P('outer', 'shard', None, 'rep'), may hold values from -6 to 6
- momentum: float32 [4, 2, 2, 128, 5120], P('outer', 'shard', None, 'rep'), may hold values from -3 to 3
Outputs:
- new_params: bfloat16 [1024, 5120], P('shard')
- new_momentum: float32 [4, 2, 2, 128, 5120], P('outer', 'shard', None, 'rep')
- new_master: float32 [4, 2, 2, 128, 5120], P('outer', 'shard', None, 'rep')
Inputs may be any that keep to these rules, and one draw needn't show every extreme that they name: `owners`: within each shard, no pod owns more than 2 blocks, and in some shards one pod owns exactly 2. `deltas`: finite values.
All inputs are finite; a program needn't handle non-finite values.
Results may differ from a plain program's by a relative error of at most 0.0075.
Values may be sent and summed in bfloat16 or wider, within the bound.
A program may use at most 128 MiB of HBM per device.

v0:
```python
import functools
import math

import jax
import jax.numpy as jnp
from jax import lax
from jax.experimental import pallas as pl
from jax.experimental.pallas import tpu as pltpu
from jax.sharding import PartitionSpec as P

CHUNKS = 4
TILE = 16
SIDE = 2


def ranks(owners, pod_count):
    owned_blocks = owners[0, :, 0]
    pod_ids = jnp.arange(pod_count, dtype=jnp.int32)
    onehot = (owned_blocks[:, None] == pod_ids[None, :]).astype(jnp.int32)
    rank_all = jnp.cumsum(onehot, axis=0) - onehot
    return owned_blocks, jnp.sum(rank_all * onehot, axis=1)


def kernel(
    chunks, rep_count, shard_count, clip_limit,
    sel, deltas, master, momentum,
    out, new_momentum, new_master,
    first, kept, passed, second, summed, third, mean, contrib, fourth, squares, others,
    send_sem, recv_sem,
):
    blocks, slots, sub_rows, width = contrib.shape[0], master.shape[0], master.shape[1], master.shape[2]
    block_rows = deltas.shape[2]
    pod_count = SIDE * SIDE
    half = width // 2
    cols = half // chunks
    o, q, s = lax.axis_index("outer"), lax.axis_index("rep"), lax.axis_index("shard")
    y, x = o // SIDE, o % SIDE
    x_pod, y_pod = y * SIDE + 1 - x, (1 - y) * SIDE + x

    def pod(d):
        return ((y + d // SIDE) % SIDE) * SIDE + (x + d % SIDE) % SIDE

    barrier = pltpu.get_barrier_semaphore()
    peers = [{"outer": pod(d)} for d in range(1, pod_count)]
    peers += [{"rep": (q + d) % rep_count} for d in range(1, rep_count)]
    peers += [{"shard": (s + d) % shard_count} for d in range(1, shard_count)]
    for peer in peers:
        pl.semaphore_signal(barrier, inc=1, device_id=peer, device_id_type=pl.DeviceIdType.MESH)
    pl.semaphore_wait(barrier, len(peers))

    started = []

    def send(src, dst, **to):
        number = len(started)
        copy = pltpu.make_async_remote_copy(
            src_ref=src, dst_ref=dst, send_sem=send_sem.at[number], recv_sem=recv_sem.at[number],
            device_id=to, device_id_type=pl.DeviceIdType.MESH,
        )
        copy.start()
        started.append(copy)
        return copy

    def tiles(rows, body):
        def step(i, carry):
            body(pl.ds(pl.multiple_of(i * TILE, TILE), TILE))
            return carry

        lax.fori_loop(0, rows // TILE, step, 0)

    def left(c):
        return pl.ds(c * cols, cols)

    def right(c):
        return pl.ds(half + c * cols, cols)

    def pair(c):
        return (left(c), right(c))

    flight = {}

    def send_first(c):
        l, r = pair(c)
        flight["first", c] = [
            send(deltas.at[:, 1 - x, :, l], first.at[:, :, l], outer=x_pod),
            send(deltas.at[1 - y, :, :, r], first.at[:, :, r], outer=y_pod),
        ]

    def send_second(c):
        for copy in flight["first", c]:
            copy.wait_recv()
        l, r = pair(c)

        def body(rows):
            for at, go, stay in ((l, 1 - y, y), (r, 1 - x, x)):
                own = (lambda k: deltas[k, x, rows, at]) if at is l else (lambda k: deltas[y, k, rows, at])
                passed[rows, at] = (
                    own(go).astype(jnp.float32) + first[go, rows, at].astype(jnp.float32)
                ).astype(jnp.bfloat16)
                kept[rows, at] = own(stay).astype(jnp.float32) + first[stay, rows, at].astype(jnp.float32)

        tiles(block_rows, body)
        flight["second", c] = [
            send(passed.at[:, l], second.at[:, l], outer=y_pod),
            send(passed.at[:, r], second.at[:, r], outer=x_pod),
        ]

    def send_third(c):
        for copy in flight["second", c]:
            copy.wait_recv()

        def body(rows):
            for at in pair(c):
                total = kept[rows, at] + second[rows, at].astype(jnp.float32)
                kept[rows, at] = total
                summed[rows, at] = total.astype(jnp.bfloat16)

        tiles(block_rows, body)
        flight["third", c] = []
        for at in pair(c):
            for d in range(1, rep_count):
                there = (q + d) % rep_count
                rows = pl.ds(pl.multiple_of(there * sub_rows, sub_rows), sub_rows)
                flight["third", c].append(send(summed.at[rows, at], third.at[d - 1, :, at], rep=there))

    def take_mean(c):
        for copy in flight["third", c]:
            copy.wait_recv()

        def body(rows):
            mine = pl.ds(pl.multiple_of(q * sub_rows + rows.start, TILE), TILE)
            for at in pair(c):
                total = kept[mine, at]
                for d in range(rep_count - 1):
                    total = total + third[d, rows, at].astype(jnp.float32)
                value = total * (1.0 / (pod_count * rep_count))
                mean[o, rows, at] = value.astype(jnp.bfloat16)
                square = value * value
                part = squares[0]
                for i in range(cols // 128):
                    for k in range(TILE // 8):
                        part = part + square[k * 8:(k + 1) * 8, i * 128:(i + 1) * 128]
                squares[0] = part

        tiles(sub_rows, body)

    def send_mean(c):
        flight["mean", c] = [
            send(mean.at[o, :, at], mean.at[o, :, at], outer=pod(d))
            for at in pair(c) for d in range(1, pod_count)
        ]

    squares[0] = jnp.zeros(squares.shape[1:], jnp.float32)
    send_first(0)
    send_first(1)
    for t in range(chunks + 2):
        if t < chunks:
            send_second(t)
        if t + 2 < chunks:
            send_first(t + 2)
        if 0 <= t - 1 < chunks:
            send_third(t - 1)
        if 0 <= t - 2 < chunks:
            take_mean(t - 2)
            if t - 2 < chunks - 1:
                send_mean(t - 2)

    number = 0
    for level, (axis, count) in enumerate((("shard", shard_count), ("rep", rep_count), ("outer", pod_count))):
        copies = []
        for d in range(1, count):
            there = {"shard": (s + d) % shard_count, "rep": (q + d) % rep_count, "outer": pod(d)}[axis]
            copies.append(send(squares.at[level], others.at[number + d - 1], **{axis: there}))
        if level == 0:
            send_mean(chunks - 1)
        total = squares[level]
        for d, copy in enumerate(copies):
            copy.wait_recv()
            total = total + others[number + d]
        number += count - 1
        squares[level + 1] = total
    total = jnp.sum(squares[3], keepdims=True)
    factor = jnp.minimum(1.0, clip_limit / jnp.sqrt(total + 1e-06))

    def update(c):
        for copy in flight["mean", c]:
            copy.wait_recv()

        def body(rows):
            for at in pair(c):
                steps = [factor * mean[b, rows, at].astype(jnp.float32) for b in range(blocks)]
                masters = []
                for j in range(slots):
                    step = sum(sel[b, j] * steps[b] for b in range(blocks))
                    moved = 0.9 * momentum[j, rows, at] + step
                    new_momentum[j, rows, at] = moved
                    value = master[j, rows, at] - 0.7 * (step + 0.9 * moved)
                    new_master[j, rows, at] = value
                    masters.append(value)
                for b in range(blocks):
                    value = sum(sel[b, j] * masters[j] for j in range(slots))
                    contrib[b, rows, at] = value.astype(jnp.bfloat16)

        tiles(sub_rows, body)
        flight["fourth", c] = []
        for at in pair(c):
            for d in range(1, pod_count):
                flight["fourth", c].append(
                    send(contrib.at[pod(d), :, at], fourth.at[d - 1, :, at], outer=pod(d))
                )

    def send_rows(c):
        for copy in flight["fourth", c]:
            copy.wait_recv()

        def body(rows):
            mine = pl.ds(pl.multiple_of(q * sub_rows + rows.start, TILE), TILE)
            for at in pair(c):
                value = contrib[o, rows, at].astype(jnp.float32)
                for d in range(pod_count - 1):
                    value = value + fourth[d, rows, at].astype(jnp.float32)
                out[y, x, mine, at] = value.astype(jnp.bfloat16)

        tiles(sub_rows, body)
        rows = pl.ds(pl.multiple_of(q * sub_rows, sub_rows), sub_rows)
        flight["rows", c] = [
            send(out.at[y, x, rows, at], out.at[y, x, rows, at], rep=(q + d) % rep_count)
            for at in pair(c) for d in range(1, rep_count)
        ]

    def send_block(c):
        for copy in flight["rows", c]:
            copy.wait_recv()
        l, r = pair(c)
        flight["block", c] = [
            send(out.at[y, x, :, l], out.at[y, x, :, l], outer=x_pod),
            send(out.at[y, x, :, r], out.at[y, x, :, r], outer=y_pod),
        ]

    def send_blocks(c):
        for copy in flight["block", c]:
            copy.wait_recv()
        l, r = pair(c)
        flight["blocks", c] = [
            send(out.at[y, :, :, l], out.at[y, :, :, l], outer=y_pod),
            send(out.at[:, x, :, r], out.at[:, x, :, r], outer=x_pod),
        ]

    for t in range(chunks + 3):
        for lag, stage in enumerate((update, send_rows, send_block, send_blocks)):
            if 0 <= t - lag < chunks:
                stage(t - lag)
    for c in range(chunks):
        for copy in flight["blocks", c]:
            copy.wait_recv()
    for copy in started:
        copy.wait_send()


def fused(deltas, owners, master, momentum):
    blocks = owners.shape[1]
    slots, sub_rows, width = master.shape[2:]
    block_rows = deltas.shape[2] // blocks
    pod_count, rep_count = lax.axis_size("outer"), lax.axis_size("rep")
    owned_blocks, rank_own = ranks(owners, pod_count)
    mine = owned_blocks == lax.axis_index("outer")
    sel = (mine[:, None] & (rank_own[:, None] == jnp.arange(slots)[None, :])).astype(jnp.float32)
    clip_limit = 0.5 * math.sqrt(lax.axis_size("shard") * blocks * block_rows * width)
    copies = CHUNKS * (4 + 2 * (rep_count - 1) + 4 * (pod_count - 1) + 2 * (rep_count - 1) + 4)
    exchanged = lax.axis_size("shard") + rep_count + pod_count - 3
    copies += exchanged
    vmem = pl.BlockSpec(memory_space=pltpu.VMEM)
    bf16, f32 = jnp.bfloat16, jnp.float32
    out, new_momentum, new_master = pl.pallas_call(
        functools.partial(kernel, CHUNKS, rep_count, lax.axis_size("shard"), clip_limit),
        out_shape=(
            jax.ShapeDtypeStruct((SIDE, SIDE, block_rows, width), bf16),
            jax.ShapeDtypeStruct(master.shape[2:], f32),
            jax.ShapeDtypeStruct(master.shape[2:], f32),
        ),
        in_specs=[pl.BlockSpec(memory_space=pltpu.SMEM), vmem, vmem, vmem],
        out_specs=(vmem, vmem, vmem),
        scratch_shapes=[
            pltpu.VMEM((SIDE, block_rows, width), bf16),
            pltpu.VMEM((block_rows, width), f32),
            pltpu.VMEM((block_rows, width), bf16),
            pltpu.VMEM((block_rows, width), bf16),
            pltpu.VMEM((block_rows, width), bf16),
            pltpu.VMEM((rep_count - 1, sub_rows, width), bf16),
            pltpu.VMEM((blocks, sub_rows, width), bf16),
            pltpu.VMEM((blocks, sub_rows, width), bf16),
            pltpu.VMEM((pod_count - 1, sub_rows, width), bf16),
            pltpu.VMEM((4, 8, 128), f32),
            pltpu.VMEM((exchanged, 8, 128), f32),
            pltpu.SemaphoreType.DMA((copies,)),
            pltpu.SemaphoreType.DMA((copies,)),
        ],
        compiler_params=pltpu.CompilerParams(
            collective_id=0, has_side_effects=True, vmem_limit_bytes=60 * 1024 * 1024
        ),
    )(
        sel,
        deltas.reshape(SIDE, SIDE, block_rows, width),
        master.reshape(master.shape[2:]),
        momentum.reshape(momentum.shape[2:]),
    )
    return (
        out.reshape(blocks * block_rows, width),
        new_momentum.reshape(momentum.shape),
        new_master.reshape(master.shape),
    )


def local(deltas, owners, master, momentum):
    blocks_here = owners.shape[1]
    slot_count = master.shape[2]
    sub_rows = master.shape[3]
    row_width = deltas.shape[3]
    block_rows = deltas.shape[2] // blocks_here
    pod_count = lax.axis_size("outer")
    rep_count = lax.axis_size("rep")
    owned_blocks = owners[0, :, 0]
    pod_ids = jnp.arange(pod_count, dtype=jnp.int32)
    onehot = (owned_blocks[:, None] == pod_ids[None, :]).astype(jnp.int32)
    rank_all = jnp.cumsum(onehot, axis=0) - onehot
    rank_own = jnp.sum(rank_all * onehot, axis=1)
    slot_ids = jnp.arange(slot_count, dtype=jnp.int32)
    selector = (
        (owned_blocks[None, None, :] == pod_ids[:, None, None])
        & (rank_own[None, None, :] == slot_ids[None, :, None])
    ).astype(jnp.bfloat16)
    local_rows = deltas[0, 0].reshape(blocks_here, block_rows, row_width)
    block_sums = lax.psum_scatter(
        local_rows.astype(jnp.float32).astype(jnp.bfloat16), "rep", scatter_dimension=1, tiled=True
    ).astype(jnp.float32)
    block_sums = block_sums.astype(jnp.bfloat16)
    pod_part = jnp.einsum(
        "ojb,brw->ojrw", selector, block_sums, preferred_element_type=jnp.float32
    ).astype(jnp.bfloat16)
    arrived = lax.all_to_all(pod_part, "outer", split_axis=0, concat_axis=0, tiled=True)
    mean_share = jnp.sum(arrived.astype(jnp.float32), axis=0) / (pod_count * rep_count)
    local_sq = jnp.sum(mean_share * mean_share)
    total_sq = lax.psum(local_sq, ("outer", "rep", "shard"))
    total_entries = lax.axis_size("shard") * blocks_here * block_rows * row_width
    clip_limit = 0.5 * math.sqrt(total_entries)
    factor = jnp.minimum(1.0, clip_limit / jnp.sqrt(total_sq + 1e-06))
    step_part = factor * mean_share[None, None]
    new_momentum = 0.9 * momentum + step_part
    new_master = master - 0.7 * (step_part + 0.9 * new_momentum)
    params_here = new_master.astype(jnp.bfloat16)
    gathered = lax.all_gather(params_here, ("outer", "rep"), axis=0, tiled=True).reshape(
        pod_count, rep_count, slot_count, sub_rows, row_width
    )
    unpacked = jnp.einsum("ojb,oqjrw->bqrw", selector, gathered, preferred_element_type=jnp.float32)
    new_params = unpacked.astype(jnp.bfloat16).reshape(blocks_here * block_rows, row_width)
    return (new_params, new_momentum, new_master)


def solution(mesh):
    fits = mesh.shape["outer"] == SIDE * SIDE

    def body(deltas, owners, master, momentum):
        blocks = owners.shape[1]
        width, sub_rows = master.shape[4], master.shape[3]
        whole = width % (2 * CHUNKS * 128) == 0 and sub_rows % TILE == 0
        plan = fused if fits and whole and blocks == SIDE * SIDE else local
        return plan(deltas, owners, master, momentum)

    return jax.shard_map(
        body,
        mesh=mesh,
        in_specs=(
            P("outer", "rep", "shard", None),
            P("shard", None, None),
            P("outer", "shard", None, "rep", None),
            P("outer", "shard", None, "rep", None),
        ),
        out_specs=(
            P("shard", None),
            P("outer", "shard", None, "rep", None),
            P("outer", "shard", None, "rep", None),
        ),
        check_vma=False,
    )
```

profile of v0, /device:TPU:0, one launch (start us, length us, event | category | flops | bytes accessed | tf_op | source)
XLA Modules:
  0.0 150.3 jit_solution(3613515182044308666)
XLA Ops:
  0.6 0.7 broadcast_compare_fusion
  1.3 0.7 fusion
  2.1 0.8 select_reduce_fusion
  2.9 0.7 fusion.2.sel
  3.6 138.6 %shard_map.67 = (bf16[2,2,128,5120]{3,2,1,0:T(8,128)(2,1)}, f32[2,32,5120]{2,1,0:T(8,128)}, f32[2,32,5120]{2,1,0:T(8,128)}) custom-call(f32[4,2]{1,0:T(4,128)} %fusion.2.sel, bf16[2,2,128,5120]{3,2,1,0:T(8,128)(2,1)} %bitcast.8, f32[2,32,5120]{2,1,0:T(8,128)} %bitcast.12, f32[2,32,5120]{2,1,0:T(8,128)} %bitcast.13), custom_call_target="tpu_custom_call" | custom-call | tf_op jit(solution)/shard_map/pallas_call | solution.py:273
  142.1 0.0 copy-start.1
  142.1 5.3 %copy.10 = bf16[512,5120]{1,0:T(8,128)(2,1)} copy(bf16[512,5120]{1,0:T(8,128)(2,1)} %bitcast.9) | data formatting | bytes 10485760
  147.4 0.0 copy-done.1
  147.4 0.0 copy-start
  147.4 1.1 copy.11
  148.5 0.7 copy-done
  149.2 1.1 copy.12
  (1 shorter events, 0.0 us)
Async XLA Ops:
  142.1 5.3 %copy-start.1 = (f32[2,32,5120]{2,1,0:T(8,128)S(1)}, f32[2,32,5120]{2,1,0:T(8,128)}, u32[]{:S(2)}) copy-start(f32[2,32,5120]{2,1,0:T(8,128)} %get-tuple-element.7) | copy-start | bytes 3932164
  147.4 1.8 %copy-start = (f32[2,32,5120]{2,1,0:T(8,128)S(1)}, f32[2,32,5120]{2,1,0:T(8,128)}, u32[]{:S(2)}) copy-start(f32[2,32,5120]{2,1,0:T(8,128)} %get-tuple-element.8) | copy-start | bytes 3932164
where the time goes:
time: 151 us; the launch traced here: 150 us
  Pallas kernels  139 us (92%)
  local copies, waits for them, and re-layouts  8.13 us (5%)
  other arithmetic  2.92 us (2%)
    pallas_call x1, Pallas kernels, fused(): pl.pallas_call(functools.partial(kernel, CHUNKS, rep_count, lax.axis_size...  139 us
    unnamed x7, local copies, waits for them, and re-layouts  8.13 us

commit v1 on v0

v1 whole, which is shorter than its diff:
```python
import functools
import math

import jax
import jax.numpy as jnp
from jax import lax
from jax.experimental import pallas as pl
from jax.experimental.pallas import tpu as pltpu
from jax.sharding import PartitionSpec as P

HALVES = 1
DEEP = 0.3
TILE = 16
SIDE = 2
LINE = 4


def kernel(
    plan, axis_sizes, clip_limit,
    owners, deltas, master, momentum,
    out, new_momentum, new_master,
    first, passed, second, zin, zrecv,
    near, far, last, onward, ztotal, cross,
    apack, arecv, mean, packed, slotted, squares, others,
    send_sem, recv_sem,
):
    halves, widths = plan
    pod_count, rep_count, shard_count = axis_sizes
    blocks, sub_rows, slots = deltas.shape[0], master.shape[1], master.shape[0]
    rows_here = sub_rows // halves
    w1, w2, w3 = widths
    pair_width = w1 + w2
    base = (0, pod_count * w1, pod_count * pair_width)
    offset = (0, w1, pair_width)
    chunks = blocks * halves
    o, q, s = lax.axis_index("outer"), lax.axis_index("rep"), lax.axis_index("shard")
    y, x = o // SIDE, o % SIDE
    neighbour = {"x": y * SIDE + 1 - x, "y": (1 - y) * SIDE + x}
    is_low = q < rep_count // 2
    tip = jnp.where(is_low, 0, rep_count - 1)
    is_tip = q == tip

    def place(k):
        return jnp.where(is_low, k, rep_count - 1 - k)

    def pod(d):
        return ((y + d // SIDE) % SIDE) * SIDE + (x + d % SIDE) % SIDE

    barrier = pltpu.get_barrier_semaphore()
    peers = []
    for d in range(pod_count):
        for e in range(rep_count):
            if d or e:
                peers.append({"outer": pod(d), "rep": (q + e) % rep_count})
    peers += [{"shard": (s + d) % shard_count} for d in range(1, shard_count)]
    for peer in peers:
        pl.semaphore_signal(barrier, inc=1, device_id=peer, device_id_type=pl.DeviceIdType.MESH)
    pl.semaphore_wait(barrier, len(peers))

    numbers, drains = {}, []

    def copy(key, src, dst, **to):
        number = numbers.setdefault(key, len(numbers))
        return pltpu.make_async_remote_copy(
            src_ref=src, dst_ref=dst, send_sem=send_sem.at[number], recv_sem=recv_sem.at[number],
            device_id=to, device_id_type=pl.DeviceIdType.MESH,
        )

    flight = {}

    def send(key, src, dst, **to):
        made = copy(key, src, dst, **to)
        made.start()
        flight[key] = made
        drains.append((None, made))

    def send_if(role, key, src, dst, **to):
        made = copy(key, src, dst, **to)
        drains.append((role, made))
        pl.when(role)(made.start)

    def arrive(key):
        flight[key].wait_recv()

    def arrive_at(key, src, dst):
        copy(key, src, dst, rep=q).wait_recv()

    def loop(count, body):
        def step(i, carry):
            body(i)
            return carry

        lax.fori_loop(0, count, step, 0)

    def up(value):
        return value.astype(jnp.float32)

    def down(value):
        return value.astype(jnp.bfloat16)

    def where(c):
        return c // halves, pl.ds((c % halves) * rows_here, rows_here)

    def cols(region, k):
        width = widths[region]
        return pl.ds(pl.multiple_of(base[region] + k * width, 128), width)

    def local_cols(region):
        return pl.ds(offset[region], widths[region])

    def order(region, c):
        return ("x", "y") if (region + c // halves) % 2 == 0 else ("y", "x")

    whole = pl.ds(base[2], pod_count * w3)

    def quarter(axis, j, away):
        if axis == "x":
            return j * SIDE + (1 - x if away else x)
        return (1 - y if away else y) * SIDE + j

    def stay(axis):
        return y if axis == "x" else x

    def send_first(c):
        b, rows = where(c)
        for r in range(2):
            axis = order(r, c)[0]
            for j in range(SIDE):
                send(
                    ("first", c, r, j), deltas.at[b, :, rows, cols(r, quarter(axis, j, True))],
                    first[r].at[j, b, :, rows, :], outer=neighbour[axis],
                )

    def send_second(c):
        b, rows = where(c)
        for r in range(2):
            axis, other = order(r, c)
            for j in range(SIDE):
                arrive(("first", c, r, j))
            go = 1 - stay(axis)
            at = cols(r, quarter(axis, go, False))

            def body(i):
                passed[r][b, i, rows, :] = down(up(deltas[b, i, rows, at]) + up(first[r][go, b, i, rows, :]))

            loop(rep_count, body)
            send(
                ("second", c, r), passed[r].at[b, :, rows, :], second[r].at[b, :, rows, :],
                outer=neighbour[other],
            )

    def send_third(c):
        b, rows = where(c)
        for r in range(2):
            axis, other = order(r, c)
            arrive(("second", c, r))
            keep = stay(axis)
            at = cols(r, o)

            def body(i):
                total = up(deltas[b, i, rows, at]) + up(first[r][keep, b, i, rows, :])
                zin[b, i, rows, local_cols(r)] = down(total + up(second[r][b, i, rows, :]))

            loop(rep_count, body)
        for d in range(1, rep_count):
            there = (q + d) % rep_count
            send(
                ("third", c, d), zin.at[b, there, rows, :], zrecv.at[d - 1, b, rows, :], rep=there
            )

    def start_tips(c):
        b, rows = where(c)
        for k in (3, 2, 1):
            send_if(
                is_tip, ("near", c, k), deltas.at[b, place(k), rows, whole], near.at[k - 1, b, rows, :],
                rep=place(1),
            )

    def relay_near(c):
        b, rows = where(c)

        @pl.when(jnp.logical_not(is_tip))
        def _():
            for k in (3, 2):
                arrive_at(("near", c, k), deltas.at[b, place(k), rows, whole], near.at[k - 1, b, rows, :])
                onward[k - 1, b, rows, :] = down(up(deltas[b, place(k), rows, whole]) + up(near[k - 1, b, rows, :]))
                copy(
                    ("far", c, 3 - k), onward.at[k - 1, b, rows, :], far.at[3 - k, b, rows, :], rep=place(2)
                ).start()

        for k in (3, 2):
            drains.append((jnp.logical_not(is_tip), copy(
                ("far", c, 3 - k), onward.at[k - 1, b, rows, :], far.at[3 - k, b, rows, :], rep=place(2)
            )))

    def relay_far(c):
        b, rows = where(c)

        @pl.when(jnp.logical_not(is_tip))
        def _():
            arrive_at(("far", c, 0), onward.at[2, b, rows, :], far.at[0, b, rows, :])
            onward[0, b, rows, :] = down(up(deltas[b, place(0), rows, whole]) + up(far[0, b, rows, :]))
            copy(("last", c), onward.at[0, b, rows, :], last.at[b, rows, :], rep=place(0)).start()

        drains.append((jnp.logical_not(is_tip), copy(
            ("last", c), onward.at[0, b, rows, :], last.at[b, rows, :], rep=place(0)
        )))

    def send_cross(c):
        b, rows = where(c)

        @pl.when(is_tip)
        def _():
            arrive_at(("last", c), onward.at[0, b, rows, :], last.at[b, rows, :])
            ztotal[b, rows, :] = down(up(deltas[b, q, rows, whole]) + up(last[b, rows, :]))

        @pl.when(jnp.logical_not(is_tip))
        def _():
            arrive_at(("near", c, 1), deltas.at[b, q, rows, whole], near.at[0, b, rows, :])
            arrive_at(("far", c, 1), onward.at[1, b, rows, :], far.at[1, b, rows, :])
            total = up(deltas[b, q, rows, whole]) + up(near[0, b, rows, :])
            ztotal[b, rows, :] = down(total + up(far[1, b, rows, :]))

        for d in range(1, pod_count):
            at = pl.ds(pl.multiple_of(pod(d) * w3, 128), w3)
            send(("cross", c, d), ztotal.at[b, rows, at], cross.at[d - 1, b, rows, :], outer=pod(d))

    scale = 1.0 / (pod_count * rep_count)

    def put_mean(b, rows, at, total):
        value = total * scale
        mean[b, rows, at] = down(value)
        square = value * value
        part = squares[0]
        height, width = square.shape
        for k in range(height // 8):
            for i in range(width // 128):
                part = part + square[k * 8:(k + 1) * 8, i * 128:(i + 1) * 128]
        squares[0] = part

    def finish_pair(c):
        b, rows = where(c)
        for d in range(1, rep_count):
            arrive(("third", c, d))
        total = up(zin[b, q, rows, :])
        for d in range(rep_count - 1):
            total = total + up(zrecv[d, b, rows, :])
        put_mean(b, rows, pl.ds(0, pair_width), total)

    def finish_cross(c):
        b, rows = where(c)
        for d in range(1, pod_count):
            arrive(("cross", c, d))
        total = up(ztotal[b, rows, pl.ds(pl.multiple_of(o * w3, 128), w3)])
        for d in range(pod_count - 1):
            total = total + up(cross[d, b, rows, :])
        put_mean(b, rows, pl.ds(pair_width, w3), total)

    owner = [owners[b] for b in range(blocks)]
    rank = []
    for b in range(blocks):
        count = jnp.int32(0)
        for before in range(b):
            count = count + (owner[before] == owner[b]).astype(jnp.int32)
        rank.append(count)

    def block_of(k, j):
        index, found = jnp.int32(0), jnp.int32(0)
        for b in range(blocks):
            match = ((owner[b] == k) & (rank[b] == j)).astype(jnp.int32)
            index, found = index + b * match, found + match
        return index, found

    def pack_early():
        for k in range(pod_count):
            for r in range(3):
                at = pl.ds(base[r] + k * widths[r], widths[r])

                def body(i):
                    value = master[i, :, at] - 0.567 * momentum[i, :, at]
                    apack[k, i, :, local_cols(r)] = down(value)

                loop(slots, body)
        arecv[o] = apack[o]

    def send_early():
        for d in range(1, pod_count):
            send(("early", d), apack.at[pod(d)], arecv.at[o], outer=pod(d))

    squares[0] = jnp.zeros(squares.shape[1:], jnp.float32)
    send_first(0)
    send_first(1)
    for c in range(chunks):
        start_tips(c)
    pack_early()
    for t in range(chunks + 3):
        if t < chunks:
            relay_near(t)
            send_second(t)
        if t + 2 < chunks:
            send_first(t + 2)
        if t == chunks - 1:
            send_early()
        if 0 <= t - 1 < chunks:
            relay_far(t - 1)
            send_third(t - 1)
        if 0 <= t - 2 < chunks:
            send_cross(t - 2)
            finish_pair(t - 2)
        if 0 <= t - 3 < chunks:
            finish_cross(t - 3)

    others[0] = jnp.sum(squares[0], axis=0, keepdims=True)
    group = pod_count * rep_count
    for d in range(pod_count):
        for e in range(rep_count):
            if d or e:
                send(
                    ("norm", d, e), others.at[0], others.at[d * rep_count + e],
                    outer=pod(d), rep=(q + e) % rep_count,
                )
    for d in range(pod_count):
        for j in range(slots):
            index = block_of(pod(d), j)[0]
            packed[d, j] = mean[index]
        if d == 0:
            slotted[o] = packed[0]
        else:
            send(("slot", d), packed.at[d], slotted.at[o], outer=pod(d))
    for d in range(pod_count):
        for e in range(rep_count):
            if d or e:
                arrive(("norm", d, e))
    total = others[0]
    for d in range(1, group):
        total = total + others[d]
    others[group] = total
    for d in range(1, shard_count):
        send(("shard", d), others.at[group], others.at[group + d], shard=(s + d) % shard_count)
    for d in range(1, pod_count):
        arrive(("early", d))
    for d in range(1, shard_count):
        arrive(("shard", d))
    for d in range(1, shard_count):
        total = total + others[group + d]
    total = jnp.sum(total, keepdims=True)
    factor = jnp.minimum(1.0, clip_limit / jnp.sqrt(total + 1e-06))

    def spread(c):
        b, rows = where(c)
        for r in range(3):
            at = local_cols(r)
            value = up(arecv[owner[b], jnp.minimum(rank[b], slots - 1), rows, at]) - (1.33 * factor) * up(mean[b, rows, at])
            out[b, q, rows, cols(r, o)] = down(value)
        for d in range(1, pod_count):
            at = out.at[b, q, rows, cols(2, o)]
            send(("wide", c, d), at, at, outer=pod(d))
        for d in range(1, rep_count):
            for r in range(2):
                at = out.at[b, q, rows, cols(r, o)]
                send(("line", c, d, r), at, at, rep=(q + d) % rep_count)

    def line(c):
        b, rows = where(c)
        for d in range(1, pod_count):
            arrive(("wide", c, d))
        mine = out.at[b, q, rows, whole]
        send_if(is_tip, ("outward", c, 0), mine, mine, rep=place(1))
        middle = jnp.logical_not(is_tip)
        send_if(middle, ("across", c, 1), mine, mine, rep=place(2))
        send_if(middle, ("inward", c, 1), mine, mine, rep=place(0))

    def line_across(c):
        b, rows = where(c)
        middle = jnp.logical_not(is_tip)
        at = out.at[b, place(0), rows, whole]
        pl.when(middle)(lambda: arrive_at(("outward", c, 0), at, at))
        send_if(middle, ("across", c, 0), at, at, rep=place(2))
        at = out.at[b, place(2), rows, whole]
        pl.when(middle)(lambda: arrive_at(("across", c, 1), at, at))
        send_if(middle, ("inward", c, 2), at, at, rep=place(0))

    def line_inward(c):
        b, rows = where(c)
        middle = jnp.logical_not(is_tip)
        at = out.at[b, place(3), rows, whole]
        pl.when(middle)(lambda: arrive_at(("across", c, 0), at, at))
        send_if(middle, ("inward", c, 3), at, at, rep=place(0))

    def line_end(c):
        b, rows = where(c)
        for k in (1, 2, 3):
            at = out.at[b, place(k), rows, whole]
            pl.when(is_tip)(lambda: arrive_at(("inward", c, k), at, at))

    def send_block(c):
        b, rows = where(c)
        for r in range(2):
            for d in range(1, rep_count):
                arrive(("line", c, d, r))
            other = order(r, c)[1]
            at = out.at[b, :, rows, cols(r, o)]
            send(("block", c, r), at, at, outer=neighbour[other])

    def send_blocks(c):
        b, rows = where(c)
        for r in range(2):
            arrive(("block", c, r))
            axis = order(r, c)[0]
            for j in range(SIDE):
                at = out.at[b, :, rows, cols(r, quarter(axis, j, False))]
                send(("blocks", c, r, j), at, at, outer=neighbour[axis])

    def update():
        for d in range(1, pod_count):
            arrive(("slot", d))
        for j in range(slots):
            found = block_of(o, j)[1].astype(jnp.float32)
            for k in range(pod_count):
                for r in range(3):
                    at = pl.ds(base[r] + k * widths[r], widths[r])
                    step = (factor * found) * up(slotted[k, j, :, local_cols(r)])
                    moved = 0.9 * momentum[j, :, at] + step
                    new_momentum[j, :, at] = moved
                    new_master[j, :, at] = master[j, :, at] - 0.7 * (step + 0.9 * moved)

    for c in range(chunks):
        spread(c)
    for t in range(chunks + 3):
        if t < chunks:
            line(t)
            send_block(t)
        if 0 <= t - 1 < chunks:
            line_across(t - 1)
            send_blocks(t - 1)
        if t == 1:
            update()
        if 0 <= t - 2 < chunks:
            line_inward(t - 2)
        if 0 <= t - 3 < chunks:
            line_end(t - 3)
    for c in range(chunks):
        for r in range(2):
            for j in range(SIDE):
                arrive(("blocks", c, r, j))
    for role, made in drains:
        if role is None:
            made.wait_send()
        else:
            pl.when(role)(made.wait_send)
    assert len(numbers) <= send_sem.shape[0]


def regions(width, pod_count):
    tiles = width // (128 * pod_count)
    third = max(1, round(tiles * DEEP))
    second = (tiles - third) // 2
    return tuple(128 * n for n in (tiles - third - second, second, third))


def fused(deltas, owners, master, momentum):
    blocks = owners.shape[1]
    slots, sub_rows, width = master.shape[2:]
    pod_count, rep_count = lax.axis_size("outer"), lax.axis_size("rep")
    shard_count = lax.axis_size("shard")
    entries = shard_count * blocks * rep_count * sub_rows * width
    clip_limit = 0.5 * math.sqrt(entries)
    widths = regions(width, pod_count)
    w1, w2, w3 = widths
    part, deep = width // pod_count, pod_count * w3
    group = pod_count * rep_count
    copies = blocks * HALVES * 39 + 2 * pod_count + group + shard_count
    vmem = pl.BlockSpec(memory_space=pltpu.VMEM)
    bf16, f32 = jnp.bfloat16, jnp.float32
    V = pltpu.VMEM
    out, new_momentum, new_master = pl.pallas_call(
        functools.partial(kernel, (HALVES, widths), (pod_count, rep_count, shard_count), clip_limit),
        out_shape=(
            V((blocks, rep_count, sub_rows, width), bf16),
            V(master.shape[2:], f32),
            V(master.shape[2:], f32),
        ),
        in_specs=[pl.BlockSpec(memory_space=pltpu.SMEM), vmem, vmem, vmem],
        out_specs=(vmem, vmem, vmem),
        scratch_shapes=[
            [V((SIDE, blocks, rep_count, sub_rows, w), bf16) for w in (w1, w2)],
            [V((blocks, rep_count, sub_rows, w), bf16) for w in (w1, w2)],
            [V((blocks, rep_count, sub_rows, w), bf16) for w in (w1, w2)],
            V((blocks, rep_count, sub_rows, w1 + w2), bf16),
            V((rep_count - 1, blocks, sub_rows, w1 + w2), bf16),
            V((3, blocks, sub_rows, deep), bf16),
            V((2, blocks, sub_rows, deep), bf16),
            V((blocks, sub_rows, deep), bf16),
            V((3, blocks, sub_rows, deep), bf16),
            V((blocks, sub_rows, deep), bf16),
            V((pod_count - 1, blocks, sub_rows, w3), bf16),
            V((pod_count, slots, sub_rows, part), bf16),
            V((pod_count, slots, sub_rows, part), bf16),
            V((blocks, sub_rows, part), bf16),
            V((pod_count, slots, sub_rows, part), bf16),
            V((pod_count, slots, sub_rows, part), bf16),
            V((1, 8, 128), f32),
            V((group + shard_count, 1, 128), f32),
            pltpu.SemaphoreType.DMA((copies,)),
            pltpu.SemaphoreType.DMA((copies,)),
        ],
        compiler_params=pltpu.CompilerParams(
            collective_id=0, has_side_effects=True, vmem_limit_bytes=48 * 1024 * 1024
        ),
    )(
        owners[0, :, 0],
        deltas.reshape(blocks, rep_count, sub_rows, width),
        master.reshape(master.shape[2:]),
        momentum.reshape(momentum.shape[2:]),
    )
    return (
        out.reshape(blocks * rep_count * sub_rows, width),
        new_momentum.reshape(momentum.shape),
        new_master.reshape(master.shape),
    )


def local(deltas, owners, master, momentum):
    blocks_here = owners.shape[1]
    slot_count = master.shape[2]
    sub_rows = master.shape[3]
    row_width = deltas.shape[3]
    block_rows = deltas.shape[2] // blocks_here
    pod_count = lax.axis_size("outer")
    rep_count = lax.axis_size("rep")
    owned_blocks = owners[0, :, 0]
    pod_ids = jnp.arange(pod_count, dtype=jnp.int32)
    onehot = (owned_blocks[:, None] == pod_ids[None, :]).astype(jnp.int32)
    rank_all = jnp.cumsum(onehot, axis=0) - onehot
    rank_own = jnp.sum(rank_all * onehot, axis=1)
    slot_ids = jnp.arange(slot_count, dtype=jnp.int32)
    selector = (
        (owned_blocks[None, None, :] == pod_ids[:, None, None])
        & (rank_own[None, None, :] == slot_ids[None, :, None])
    ).astype(jnp.bfloat16)
    local_rows = deltas[0, 0].reshape(blocks_here, block_rows, row_width)
    block_sums = lax.psum_scatter(
        local_rows.astype(jnp.float32).astype(jnp.bfloat16), "rep", scatter_dimension=1, tiled=True
    ).astype(jnp.float32)
    block_sums = block_sums.astype(jnp.bfloat16)
    pod_part = jnp.einsum(
        "ojb,brw->ojrw", selector, block_sums, preferred_element_type=jnp.float32
    ).astype(jnp.bfloat16)
    arrived = lax.all_to_all(pod_part, "outer", split_axis=0, concat_axis=0, tiled=True)
    mean_share = jnp.sum(arrived.astype(jnp.float32), axis=0) / (pod_count * rep_count)
    local_sq = jnp.sum(mean_share * mean_share)
    total_sq = lax.psum(local_sq, ("outer", "rep", "shard"))
    total_entries = lax.axis_size("shard") * blocks_here * block_rows * row_width
    clip_limit = 0.5 * math.sqrt(total_entries)
    factor = jnp.minimum(1.0, clip_limit / jnp.sqrt(total_sq + 1e-06))
    step_part = factor * mean_share[None, None]
    new_momentum = 0.9 * momentum + step_part
    new_master = master - 0.7 * (step_part + 0.9 * new_momentum)
    params_here = new_master.astype(jnp.bfloat16)
    gathered = lax.all_gather(params_here, ("outer", "rep"), axis=0, tiled=True).reshape(
        pod_count, rep_count, slot_count, sub_rows, row_width
    )
    unpacked = jnp.einsum("ojb,oqjrw->bqrw", selector, gathered, preferred_element_type=jnp.float32)
    new_params = unpacked.astype(jnp.bfloat16).reshape(blocks_here * block_rows, row_width)
    return (new_params, new_momentum, new_master)


def solution(mesh):
    fits = mesh.shape["outer"] == SIDE * SIDE and mesh.shape["rep"] == LINE

    def body(deltas, owners, master, momentum):
        blocks = owners.shape[1]
        width, sub_rows = master.shape[4], master.shape[3]
        tiled = width % (SIDE * SIDE * 128) == 0 and width >= 3 * SIDE * SIDE * 128
        tiled = tiled and sub_rows % (TILE * HALVES) == 0
        tiled = tiled and deltas.shape[2] == blocks * LINE * sub_rows
        return (fused if fits and tiled else local)(deltas, owners, master, momentum)

    return jax.shard_map(
        body,
        mesh=mesh,
        in_specs=(
            P("outer", "rep", "shard", None),
            P("shard", None, None),
            P("outer", "shard", None, "rep", None),
            P("outer", "shard", None, "rep", None),
        ),
        out_specs=(
            P("shard", None),
            P("outer", "shard", None, "rep", None),
            P("outer", "shard", None, "rep", None),
        ),
        check_vma=False,
    )
```

time: 151 us -> 121 us (0.80)
  Pallas kernels: 139 us -> 115 us
  local copies, waits for them, and re-layouts: 8.13 us -> 4.47 us
  other arithmetic: 2.92 us -> 0 us
    pallas_call x1, Pallas kernels: 139 us -> 115 us  [fused(): pl.pallas_call(functools.partial(kernel, (HALVES, widths), (pod_count, re...]
    unnamed x7 -> x3, local copies, waits for them, and re-layouts: 8.13 us -> 4.47 us
where the time goes in v1:
time: 121 us; the launch traced here: 120 us
  Pallas kernels  115 us (95%)
  local copies, waits for them, and re-layouts  4.47 us (4%)
    pallas_call x1, Pallas kernels, fused(): pl.pallas_call(functools.partial(kernel, (HALVES, widths), (pod_count, re...  115 us
    unnamed x3, local copies, waits for them, and re-layouts  4.47 us

profile of v1, /device:TPU:0, one launch (start us, length us, event | category | flops | bytes accessed | tf_op | source)
XLA Modules:
  0.0 120.0 jit_solution(6895243760106326546)
XLA Ops:
  0.6 114.9 %shard_map.67 = (bf16[4,4,32,5120]{3,2,1,0:T(8,128)(2,1)S(1)}, f32[2,32,5120]{2,1,0:T(8,128)S(1)}, f32[2,32,5120]{2,1,0:T(8,128)S(1)}) custom-call(s32[4]{0:T(128)} %bitcast.13, bf16[4,4,32,5120]{3,2,1,0:T(8,128)(2,1)} %bitcast.10, f32[2,32,5120]{2,1,0:T(8,128)} %bitcast.11, f32[2,32,5120]{2,1,0:T(8,128)} %bitcast.12), custom_call_target="tpu_custom_call" | custom-call | tf_op jit(solution)/shard_map/pallas_call | solution.py:476
  115.5 2.4 %copy.10 = bf16[512,5120]{1,0:T(8,128)(2,1)} copy(bf16[512,5120]{1,0:T(8,128)(2,1)S(1)} %bitcast.7) | data formatting | bytes 10485760
  117.9 1.1 copy.11
  119.0 1.1 copy.12

commit v2 on v1

v2 whole, which is shorter than its diff:
```python
import functools
import math

import jax
import jax.numpy as jnp
from jax import lax
from jax.experimental import pallas as pl
from jax.experimental.pallas import tpu as pltpu
from jax.sharding import PartitionSpec as P

DEEP_IN = 0.3
DEEP_OUT = 0.2
TILE = 16
SIDE = 2
LATE = 2
KINDS = 18
LINE = 4


def kernel(
    plan, axis_sizes, clip_limit,
    owners_far, deltas_far, master_far, momentum_far,
    out, new_momentum, new_master,
    owners, deltas, master, momentum, load_sem, first, passed, second, zin, zrecv,
    staged, near, far, last, onward, ztotal, cross,
    apack, arecv, mean, packed, slotted, squares, others,
    send_sem, recv_sem,
):
    wa, wb, wc, ws = plan
    pod_count, rep_count, shard_count = axis_sizes
    blocks, sub_rows, slots = deltas.shape[0], master.shape[1], master.shape[0]
    widths = (wa, wb, wc)
    base = (0, pod_count * wa, pod_count * (wa + wb))
    offset = (0, wa, wa + wb)
    pair = (wa, ws)
    pair_width, deep_width = wa + ws, wb - ws + wc
    o, q, s = lax.axis_index("outer"), lax.axis_index("rep"), lax.axis_index("shard")
    y, x = o // SIDE, o % SIDE
    neighbour = {"x": y * SIDE + 1 - x, "y": (1 - y) * SIDE + x}
    is_low = q < rep_count // 2
    tip = jnp.where(is_low, 0, rep_count - 1)
    is_tip = q == tip

    def place(k):
        return jnp.where(is_low, k, rep_count - 1 - k)

    def pod(d):
        return ((y + d // SIDE) % SIDE) * SIDE + (x + d % SIDE) % SIDE

    barrier = pltpu.get_barrier_semaphore()
    peers = []
    for d in range(pod_count):
        for e in range(rep_count):
            if d or e:
                peers.append({"outer": pod(d), "rep": (q + e) % rep_count})
    peers += [{"shard": (s + d) % shard_count} for d in range(1, shard_count)]
    for peer in peers:
        pl.semaphore_signal(barrier, inc=1, device_id=peer, device_id_type=pl.DeviceIdType.MESH)
    loads = [
        pltpu.make_async_copy(deltas_far.at[b], deltas.at[b], load_sem.at[b]) for b in range(blocks)
    ]
    loads.append(pltpu.make_async_copy(master_far, master, load_sem.at[blocks]))
    loads.append(pltpu.make_async_copy(momentum_far, momentum, load_sem.at[blocks + 1]))
    loads.append(pltpu.make_async_copy(owners_far, owners, load_sem.at[blocks + 2]))
    for load in loads:
        load.start()
    pl.semaphore_wait(barrier, len(peers))

    numbers, sent, roles = {}, {}, {}

    def copy(group, src, dst, **to):
        kind = group[0]
        number = numbers.setdefault(group, len(numbers))
        sent.setdefault(kind, len(sent))
        return pltpu.make_async_remote_copy(
            src_ref=src, dst_ref=dst, send_sem=send_sem.at[sent[kind]], recv_sem=recv_sem.at[number],
            device_id=to, device_id_type=pl.DeviceIdType.MESH,
        )

    def send(group, src, dst, **to):
        roles[group[0]] = None
        copy(group, src, dst, **to).start()

    def send_if(role, group, src, dst, **to):
        roles[group[0]] = role
        pl.when(role)(copy(group, src, dst, **to).start)

    def arrive(group, like):
        copy(group, like, like, rep=q).wait_recv()

    def leave(kind, like):
        made = pltpu.make_async_remote_copy(
            src_ref=like, dst_ref=like, send_sem=send_sem.at[sent[kind]], recv_sem=recv_sem.at[0],
            device_id={"rep": q}, device_id_type=pl.DeviceIdType.MESH,
        )
        if roles[kind] is None:
            made.wait_send()
        else:
            pl.when(roles[kind])(made.wait_send)

    def loop(count, body):
        def step(i, carry):
            body(i)
            return carry

        lax.fori_loop(0, count, step, 0)

    def up(value):
        return value.astype(jnp.float32)

    def down(value):
        return value.astype(jnp.bfloat16)

    def cols(region, k):
        width = widths[region]
        return pl.ds(pl.multiple_of(base[region] + k * width, 128), width)

    def pair_cols(r, k):
        return pl.ds(pl.multiple_of(base[r] + k * widths[r], 128), pair[r])

    def local_cols(region):
        return pl.ds(offset[region], widths[region])

    def pair_local(r):
        return pl.ds(offset[r], pair[r])

    def deep_cols(k):
        return pl.ds(pl.multiple_of(k * deep_width, 128), deep_width)

    def order(region, b):
        return ("x", "y") if (region + b) % 2 == 0 else ("y", "x")

    def at_rows(g):
        return slice(None) if g is None else (q + g) % rep_count

    def each(g, body):
        if g is None:
            loop(rep_count, body)
        else:
            body((q + g) % rep_count)

    tail = (None,)
    others_of = tuple(range(1, rep_count))

    def late(b):
        return b >= blocks - LATE

    whole = pl.ds(base[2], pod_count * wc)

    def quarter(axis, j, away):
        if axis == "x":
            return j * SIDE + (1 - x if away else x)
        return (1 - y if away else y) * SIDE + j

    def stay(axis):
        return y if axis == "x" else x

    def send_first(b, g):
        i = at_rows(g)
        for r in range(2):
            axis = order(r, b)[0]
            for j in range(SIDE):
                send(
                    ("first", b, g), deltas.at[b, i, :, pair_cols(r, quarter(axis, j, True))],
                    first[r].at[j, b, i], outer=neighbour[axis],
                )

    def send_second(b, g):
        arrive(("first", b, g), deltas.at[b, at_rows(g), :, pl.ds(0, SIDE * pair_width)])
        for r in range(2):
            axis, other = order(r, b)
            go = 1 - stay(axis)
            at = pair_cols(r, quarter(axis, go, False))

            def body(i):
                passed[r][b, i] = down(up(deltas[b, i, :, at]) + up(first[r][go, b, i]))

            each(g, body)
            i = at_rows(g)
            send(("second", b, g), passed[r].at[b, i], second[r].at[b, i], outer=neighbour[other])

    def pair_total(r, b, i):
        total = up(deltas[b, i, :, pair_cols(r, o)]) + up(first[r][stay(order(r, b)[0]), b, i])
        return total + up(second[r][b, i])

    def send_third(b):
        groups = others_of if late(b) else tail
        for g in groups:
            arrive(("second", b, g), deltas.at[b, at_rows(g), :, pl.ds(0, pair_width)])
        for d in others_of:
            there = (q + d) % rep_count
            for r in range(2):
                zin[b, d - 1, :, pair_local(r)] = down(pair_total(r, b, there))
            send(("third", b), zin.at[b, d - 1], zrecv.at[d - 1, b], rep=there)

    def deep_of(b, i):
        parts = []
        for k in range(pod_count):
            parts.append(deltas[b, i, :, pl.ds(base[1] + k * wb + ws, wb - ws)])
            parts.append(deltas[b, i, :, pl.ds(base[2] + k * wc, wc)])
        return jnp.concatenate([p for p in parts if p.shape[-1]], axis=-1)

    def start_tips(b):
        @pl.when(is_tip)
        def _():
            for k in (3, 2, 1):
                staged[k - 1, b] = deep_of(b, place(k))
                copy(("near", b, k), staged.at[k - 1, b], near.at[k - 1, b], rep=place(1)).start()

        roles["near"] = is_tip

    def relay_near(b):
        @pl.when(jnp.logical_not(is_tip))
        def _():
            for k in (3, 2):
                arrive(("near", b, k), near.at[k - 1, b])
                onward[k - 1, b] = down(up(deep_of(b, place(k))) + up(near[k - 1, b]))
                copy(("far", b, 3 - k), onward.at[k - 1, b], far.at[3 - k, b], rep=place(2)).start()

        roles["far"] = jnp.logical_not(is_tip)

    def relay_far(b):
        @pl.when(jnp.logical_not(is_tip))
        def _():
            arrive(("far", b, 0), far.at[0, b])
            onward[0, b] = down(up(deep_of(b, place(0))) + up(far[0, b]))
            copy(("last", b), onward.at[0, b], last.at[b], rep=place(0)).start()

        roles["last"] = jnp.logical_not(is_tip)

    def send_cross(b):
        @pl.when(is_tip)
        def _():
            arrive(("last", b), last.at[b])
            ztotal[b] = down(up(deep_of(b, q)) + up(last[b]))

        @pl.when(jnp.logical_not(is_tip))
        def _():
            arrive(("near", b, 1), near.at[0, b])
            arrive(("far", b, 1), far.at[1, b])
            ztotal[b] = down(up(deep_of(b, q)) + up(near[0, b]) + up(far[1, b]))

        for d in range(1, pod_count):
            send(("cross", b), ztotal.at[b, :, deep_cols(pod(d))], cross.at[d - 1, b], outer=pod(d))

    scale = 1.0 / (pod_count * rep_count)

    def put_mean(b, at, total):
        value = total * scale
        mean[b, :, at] = down(value)
        square = value * value
        part = squares[0]
        height, width = square.shape
        for k in range(height // 8):
            for i in range(width // 128):
                part = part + square[k * 8:(k + 1) * 8, i * 128:(i + 1) * 128]
        squares[0] = part

    def finish_pair(b):
        if late(b):
            arrive(("second", b, 0), deltas.at[b, q, :, pl.ds(0, pair_width)])
        arrive(("third", b), zrecv.at[:, b])
        for r in range(2):
            total = pair_total(r, b, q)
            for d in range(rep_count - 1):
                total = total + up(zrecv[d, b, :, pair_local(r)])
            put_mean(b, pair_local(r), total)

    def finish_cross(b):
        arrive(("cross", b), cross.at[:, b])
        total = up(ztotal[b, :, deep_cols(o)])
        for d in range(pod_count - 1):
            total = total + up(cross[d, b])
        put_mean(b, pl.ds(pair_width, deep_width), total)

    owner, rank = [], []

    def read_owners():
        loads[blocks + 2].wait()
        owner.extend(owners[b] for b in range(blocks))
        for b in range(blocks):
            count = jnp.int32(0)
            for before in range(b):
                count = count + (owner[before] == owner[b]).astype(jnp.int32)
            rank.append(count)

    def block_of(k, j):
        index, found = jnp.int32(0), jnp.int32(0)
        for b in range(blocks):
            match = ((owner[b] == k) & (rank[b] == j)).astype(jnp.int32)
            index, found = index + b * match, found + match
        return index, found

    def load_rows(b):
        loads[b].wait()

    def pack_early():
        loads[blocks].wait()
        loads[blocks + 1].wait()
        for k in range(pod_count):
            for r in range(3):
                at = pl.ds(base[r] + k * widths[r], widths[r])

                def body(i):
                    value = master[i, :, at] - 0.567 * momentum[i, :, at]
                    apack[k, i, :, local_cols(r)] = down(value)

                loop(slots, body)
        arecv[o] = apack[o]

    def send_early():
        for d in range(1, pod_count):
            send(("early",), apack.at[pod(d)], arecv.at[o], outer=pod(d))

    group = pod_count * rep_count

    def norm_send():
        others[0] = jnp.sum(squares[0], axis=0, keepdims=True)
        for d in range(pod_count):
            for e in range(rep_count):
                if d or e:
                    send(
                        ("norm",), others.at[0], others.at[d * rep_count + e],
                        outer=pod(d), rep=(q + e) % rep_count,
                    )

    def mean_send():
        for d in range(pod_count):
            for j in range(slots):
                index = block_of(pod(d), j)[0]
                packed[d, j] = mean[index]
            if d == 0:
                slotted[o] = packed[0]
            else:
                send(("slot",), packed.at[d], slotted.at[o], outer=pod(d))

    def norm_wait():
        arrive(("norm",), others.at[pl.ds(1, group - 1)])
        total = others[0]
        for d in range(1, group):
            total = total + others[d]
        others[group] = total
        for d in range(1, shard_count):
            send(("shard",), others.at[group], others.at[group + d], shard=(s + d) % shard_count)
        arrive(("early",), arecv.at[pl.ds(1, pod_count - 1)])

    def norm_shard():
        arrive(("shard",), others.at[pl.ds(group + 1, shard_count - 1)])
        total = others[group]
        for d in range(1, shard_count):
            total = total + others[group + d]
        total = jnp.sum(total, keepdims=True)
        return jnp.minimum(1.0, clip_limit / jnp.sqrt(total + 1e-06))

    def spread(b, factor):
        for r in range(3):
            at = local_cols(r)
            early = up(arecv[owner[b], jnp.minimum(rank[b], slots - 1), :, at])
            value = early - (1.33 * factor) * up(mean[b, :, at])
            out[b, q, :, cols(r, o)] = down(value)

    def send_wide(b):
        for d in range(1, pod_count):
            at = out.at[b, q, :, cols(2, o)]
            send(("wide", b), at, at, outer=pod(d))

    def send_line(b):
        for d in others_of:
            for r in range(2):
                at = out.at[b, q, :, cols(r, o)]
                send(("line", b, d), at, at, rep=(q + d) % rep_count)

    middle = jnp.logical_not(is_tip)

    def line(b):
        arrive(("wide", b), out.at[b, q, :, pl.ds(0, (pod_count - 1) * wc)])
        mine = out.at[b, q, :, whole]
        send_if(is_tip, ("outward", b, 0), mine, mine, rep=place(1))
        send_if(middle, ("across", b, 1), mine, mine, rep=place(2))
        send_if(middle, ("inward",), mine, mine, rep=place(0))

    def line_across(b):
        at = out.at[b, place(0), :, whole]
        pl.when(middle)(lambda: arrive(("outward", b, 0), at))
        send_if(middle, ("across", b, 0), at, at, rep=place(2))
        at2 = out.at[b, place(2), :, whole]
        pl.when(middle)(lambda: arrive(("across", b, 1), at2))
        send_if(middle, ("inward",), at2, at2, rep=place(0))

    def line_inward(b):
        at = out.at[b, place(3), :, whole]
        pl.when(middle)(lambda: arrive(("across", b, 0), at))
        send_if(middle, ("inward",), at, at, rep=place(0))

    def line_end():
        pl.when(is_tip)(lambda: arrive(("inward",), out.at[:, pl.ds(0, 3), :, whole]))

    def send_block(b, d):
        i = (q + rep_count - d) % rep_count
        if d:
            arrive(("line", b, d), out.at[b, i, :, pl.ds(0, wa + wb)])
        for r in range(2):
            at = out.at[b, i, :, cols(r, o)]
            send(("block", b, d), at, at, outer=neighbour[order(r, b)[1]])

    def send_blocks(b, d):
        i = (q + rep_count - d) % rep_count
        arrive(("block", b, d), out.at[b, i, :, pl.ds(0, wa + wb)])
        for r in range(2):
            axis = order(r, b)[0]
            for j in range(SIDE):
                at = out.at[b, i, :, cols(r, quarter(axis, j, False))]
                send(("blocks",), at, at, outer=neighbour[axis])

    def update(factor):
        arrive(("slot",), slotted.at[pl.ds(1, pod_count - 1)])
        for j in range(slots):
            found = block_of(o, j)[1].astype(jnp.float32)
            for k in range(pod_count):
                for r in range(3):
                    at = pl.ds(base[r] + k * widths[r], widths[r])
                    step = (factor * found) * up(slotted[k, j, :, local_cols(r)])
                    moved = 0.9 * momentum[j, :, at] + step
                    new_momentum[j, :, at] = moved
                    new_master[j, :, at] = master[j, :, at] - 0.7 * (step + 0.9 * moved)

    def finish():
        arrive(("blocks",), out.at[:, :, :, pl.ds(0, SIDE * (wa + wb))])

    def drain():
        leave("first", deltas.at[:, :, :, pl.ds(0, SIDE * pair_width)])
        leave("second", deltas.at[:, :, :, pl.ds(0, pair_width)])
        leave("third", zin)
        leave("near", staged)
        leave("far", far)
        leave("last", last)
        leave("cross", cross)
        leave("early", arecv.at[pl.ds(1, pod_count - 1)])
        leave("norm", others.at[pl.ds(1, group - 1)])
        leave("slot", slotted.at[pl.ds(1, pod_count - 1)])
        leave("shard", others.at[pl.ds(group + 1, shard_count - 1)])
        leave("wide", out.at[:, 0, :, pl.ds(0, (pod_count - 1) * wc)])
        leave("line", out.at[:, pl.ds(0, rep_count - 1), :, pl.ds(0, wa + wb)])
        leave("outward", out.at[:, 0, :, whole])
        leave("across", out.at[:, pl.ds(0, 2), :, whole])
        leave("inward", out.at[:, pl.ds(0, 3), :, whole])
        leave("block", out.at[:, :, :, pl.ds(0, wa + wb)])
        leave("blocks", out.at[:, :, :, pl.ds(0, SIDE * (wa + wb))])

    squares[0] = jnp.zeros(squares.shape[1:], jnp.float32)
    def firsts(b):
        for g in others_of if late(b) else tail:
            send_first(b, g)

    def seconds(b):
        for g in others_of if late(b) else tail:
            send_second(b, g)

    for b in range(blocks):
        load_rows(b)
        if b < 2:
            firsts(b)
        if b > 0:
            start_tips(b - 1)
    start_tips(blocks - 1)
    pack_early()
    read_owners()
    for t in range(blocks + 2):
        if t < blocks:
            relay_near(t)
            seconds(t)
        if t + 2 < blocks:
            firsts(t + 2)
            if t + 3 == blocks:
                for b in range(blocks - LATE, blocks):
                    send_first(b, 0)
        if 0 <= t - 1 < blocks:
            if t == blocks:
                send_early()
                for b in range(blocks - LATE, blocks):
                    send_second(b, 0)
                send_third(t - 1)
                relay_far(t - 1)
            else:
                relay_far(t - 1)
                send_third(t - 1)
        if 0 <= t - 2 < blocks:
            send_cross(t - 2)
    for b in range(blocks):
        finish_pair(b)
        finish_cross(b)
    norm_send()
    mean_send()
    norm_wait()
    factor = norm_shard()
    for b in range(blocks):
        spread(b, factor)
        send_wide(b)
        send_block(b, 0)
        if b == 0:
            send_line(0)
    for b in range(blocks):
        line(b)
        for later in {0: (1,), 1: (2, 3)}.get(b, ()):
            send_line(later)
    for b in range(blocks):
        send_blocks(b, 0)
    for b in range(blocks):
        for d in others_of:
            send_block(b, d)
        line_across(b)
        for d in others_of:
            send_blocks(b, d)
        if b == 1:
            update(factor)
    for b in range(blocks):
        line_inward(b)
    line_end()
    finish()
    drain()
    assert len(numbers) == recv_sem.shape[0] and len(sent) == send_sem.shape[0]


def store(*refs):
    sem = refs[-1]
    copies = [pltpu.make_async_copy(refs[i], refs[i + 3], sem.at[i]) for i in range(3)]
    for copy in copies:
        copy.start()
    for copy in copies:
        copy.wait()


def regions(width, pod_count):
    tiles = width // (128 * pod_count)
    deep = round(tiles * DEEP_IN)
    wc = min(deep, round(tiles * DEEP_OUT))
    wb = (tiles - wc) // 2
    return tuple(128 * n for n in (tiles - wc - wb, wb, wc, wb - (deep - wc)))


def fused(deltas, owners, master, momentum):
    blocks = owners.shape[1]
    slots, sub_rows, width = master.shape[2:]
    pod_count, rep_count = lax.axis_size("outer"), lax.axis_size("rep")
    shard_count = lax.axis_size("shard")
    entries = shard_count * blocks * rep_count * sub_rows * width
    clip_limit = 0.5 * math.sqrt(entries)
    widths = regions(width, pod_count)
    wa, wb, wc, ws = widths
    part, deep_width = width // pod_count, wb - ws + wc
    deep = pod_count * deep_width
    group = pod_count * rep_count
    waits = 2 * (blocks + (rep_count - 1) * LATE) + 8 * blocks + 4 + blocks * (2 * rep_count + 3) + 2
    vmem, hbm = pl.BlockSpec(memory_space=pltpu.VMEM), pl.BlockSpec(memory_space=pltpu.HBM)
    bf16, f32 = jnp.bfloat16, jnp.float32
    V = pltpu.VMEM
    out, new_momentum, new_master = pl.pallas_call(
        functools.partial(kernel, widths, (pod_count, rep_count, shard_count), clip_limit),
        out_shape=(
            V((blocks, rep_count, sub_rows, width), bf16),
            V(master.shape[2:], f32),
            V(master.shape[2:], f32),
        ),
        in_specs=[hbm] * 4,
        out_specs=(vmem, vmem, vmem),
        scratch_shapes=[
            pltpu.SMEM((blocks,), jnp.int32),
            V((blocks, rep_count, sub_rows, width), bf16),
            V(master.shape[2:], f32),
            V(master.shape[2:], f32),
            pltpu.SemaphoreType.DMA((blocks + 3,)),
            [V((SIDE, blocks, rep_count, sub_rows, w), bf16) for w in (wa, ws)],
            [V((blocks, rep_count, sub_rows, w), bf16) for w in (wa, ws)],
            [V((blocks, rep_count, sub_rows, w), bf16) for w in (wa, ws)],
            V((blocks, rep_count - 1, sub_rows, wa + ws), bf16),
            V((rep_count - 1, blocks, sub_rows, wa + ws), bf16),
            V((3, blocks, sub_rows, deep), bf16),
            V((3, blocks, sub_rows, deep), bf16),
            V((2, blocks, sub_rows, deep), bf16),
            V((blocks, sub_rows, deep), bf16),
            V((3, blocks, sub_rows, deep), bf16),
            V((blocks, sub_rows, deep), bf16),
            V((pod_count - 1, blocks, sub_rows, deep_width), bf16),
            V((pod_count, slots, sub_rows, part), bf16),
            V((pod_count, slots, sub_rows, part), bf16),
            V((blocks, sub_rows, part), bf16),
            V((pod_count, slots, sub_rows, part), bf16),
            V((pod_count, slots, sub_rows, part), bf16),
            V((1, 8, 128), f32),
            V((group + shard_count, 1, 128), f32),
            pltpu.SemaphoreType.DMA((KINDS,)),
            pltpu.SemaphoreType.DMA((waits,)),
        ],
        compiler_params=pltpu.CompilerParams(
            collective_id=0, has_side_effects=True, vmem_limit_bytes=48 * 1024 * 1024
        ),
    )(
        owners[0, :, 0],
        deltas.reshape(blocks, rep_count, sub_rows, width),
        master.reshape(master.shape[2:]),
        momentum.reshape(momentum.shape[2:]),
    )
    arrays = (out, new_momentum, new_master)
    out, new_momentum, new_master = pl.pallas_call(
        store,
        out_shape=tuple(jax.ShapeDtypeStruct(a.shape, a.dtype) for a in arrays),
        in_specs=[pl.BlockSpec(memory_space=pl.ANY)] * 3,
        out_specs=(hbm,) * 3,
        scratch_shapes=[pltpu.SemaphoreType.DMA((3,))],
        compiler_params=pltpu.CompilerParams(vmem_limit_bytes=4 * 1024 * 1024),
    )(*(pltpu.with_memory_space_constraint(a, pltpu.VMEM) for a in arrays))
    return (
        out.reshape(blocks * rep_count * sub_rows, width),
        new_momentum.reshape(momentum.shape),
        new_master.reshape(master.shape),
    )


def local(deltas, owners, master, momentum):
    blocks_here = owners.shape[1]
    slot_count = master.shape[2]
    sub_rows = master.shape[3]
    row_width = deltas.shape[3]
    block_rows = deltas.shape[2] // blocks_here
    pod_count = lax.axis_size("outer")
    rep_count = lax.axis_size("rep")
    owned_blocks = owners[0, :, 0]
    pod_ids = jnp.arange(pod_count, dtype=jnp.int32)
    onehot = (owned_blocks[:, None] == pod_ids[None, :]).astype(jnp.int32)
    rank_all = jnp.cumsum(onehot, axis=0) - onehot
    rank_own = jnp.sum(rank_all * onehot, axis=1)
    slot_ids = jnp.arange(slot_count, dtype=jnp.int32)
    selector = (
        (owned_blocks[None, None, :] == pod_ids[:, None, None])
        & (rank_own[None, None, :] == slot_ids[None, :, None])
    ).astype(jnp.bfloat16)
    local_rows = deltas[0, 0].reshape(blocks_here, block_rows, row_width)
    block_sums = lax.psum_scatter(
        local_rows.astype(jnp.float32).astype(jnp.bfloat16), "rep", scatter_dimension=1, tiled=True
    ).astype(jnp.float32)
    block_sums = block_sums.astype(jnp.bfloat16)
    pod_part = jnp.einsum(
        "ojb,brw->ojrw", selector, block_sums, preferred_element_type=jnp.float32
    ).astype(jnp.bfloat16)
    arrived = lax.all_to_all(pod_part, "outer", split_axis=0, concat_axis=0, tiled=True)
    mean_share = jnp.sum(arrived.astype(jnp.float32), axis=0) / (pod_count * rep_count)
    local_sq = jnp.sum(mean_share * mean_share)
    total_sq = lax.psum(local_sq, ("outer", "rep", "shard"))
    total_entries = lax.axis_size("shard") * blocks_here * block_rows * row_width
    clip_limit = 0.5 * math.sqrt(total_entries)
    factor = jnp.minimum(1.0, clip_limit / jnp.sqrt(total_sq + 1e-06))
    step_part = factor * mean_share[None, None]
    new_momentum = 0.9 * momentum + step_part
    new_master = master - 0.7 * (step_part + 0.9 * new_momentum)
    params_here = new_master.astype(jnp.bfloat16)
    gathered = lax.all_gather(params_here, ("outer", "rep"), axis=0, tiled=True).reshape(
        pod_count, rep_count, slot_count, sub_rows, row_width
    )
    unpacked = jnp.einsum("ojb,oqjrw->bqrw", selector, gathered, preferred_element_type=jnp.float32)
    new_params = unpacked.astype(jnp.bfloat16).reshape(blocks_here * block_rows, row_width)
    return (new_params, new_momentum, new_master)


def solution(mesh):
    fits = mesh.shape["outer"] == SIDE * SIDE and mesh.shape["rep"] == LINE

    def body(deltas, owners, master, momentum):
        blocks = owners.shape[1]
        width, sub_rows = master.shape[4], master.shape[3]
        tiled = width % (SIDE * SIDE * 128) == 0 and width >= 3 * SIDE * SIDE * 128
        tiled = tiled and sub_rows % TILE == 0 and blocks == SIDE * SIDE
        tiled = tiled and deltas.shape[2] == blocks * LINE * sub_rows
        return (fused if fits and tiled else local)(deltas, owners, master, momentum)

    return jax.shard_map(
        body,
        mesh=mesh,
        in_specs=(
            P("outer", "rep", "shard", None),
            P("shard", None, None),
            P("outer", "shard", None, "rep", None),
            P("outer", "shard", None, "rep", None),
        ),
        out_specs=(
            P("shard", None),
            P("outer", "shard", None, "rep", None),
            P("outer", "shard", None, "rep", None),
        ),
        check_vma=False,
    )
```

time: 121 us -> 104 us (0.86)
  Pallas kernels: 115 us -> 103 us
  local copies, waits for them, and re-layouts: 4.47 us -> 0 us
    pallas_call x1 -> x2, Pallas kernels: 115 us -> 103 us  [the longest x1 100 us: fused(): pl.pallas_call(functools.partial(kernel, widths, (pod_count, rep_count, s...]
    unnamed x3 -> x0, local copies, waits for them, and re-layouts: 4.47 us -> none
where the time goes in v2:
time: 104 us
  Pallas kernels  103 us (99%)
    pallas_call x1, Pallas kernels, fused(): pl.pallas_call(functools.partial(kernel, widths, (pod_count, rep_count, s...  100 us
    pallas_call x1, Pallas kernels, fused(): pl.pallas_call(store, out_shape=tuple((jax.ShapeDtypeStruct(a.shape, a.dt...  3.2 us

profile of v2, /device:TPU:0, one launch (start us, length us, event | category | flops | bytes accessed | tf_op | source)
XLA Modules:
  0.0 104.1 jit_solution(4720100934543803036)
XLA Ops:
  0.6 100.2 %shard_map.67 = (bf16[4,4,32,5120]{3,2,1,0:T(8,128)(2,1)S(1)}, f32[2,32,5120]{2,1,0:T(8,128)S(1)}, f32[2,32,5120]{2,1,0:T(8,128)S(1)}) custom-call(s32[4]{0:T(128)} %bitcast.10, bf16[4,4,32,5120]{3,2,1,0:T(8,128)(2,1)} %bitcast.7, f32[2,32,5120]{2,1,0:T(8,128)} %bitcast.8, f32[2,32,5120]{2,1,0:T(8,128)} %bitcast.9), custom_call_target="tpu_custom_call" | custom-call | tf_op jit(solution)/shard_map/pallas_call | solution.py:557
  100.9 3.2 %shard_map.68 = (bf16[4,4,32,5120]{3,2,1,0:T(8,128)(2,1)}, f32[2,32,5120]{2,1,0:T(8,128)}, f32[2,32,5120]{2,1,0:T(8,128)}) custom-call(bf16[4,4,32,5120]{3,2,1,0:T(8,128)(2,1)S(1)} %get-tuple-element.9.refs_0_, f32[2,32,5120]{2,1,0:T(8,128)S(1)} %get-tuple-element.10.refs_1_, f32[2,32,5120]{2,1,0:T(8,128)S(1)} %get-tuple-element.11.refs_2_), custom_call_target="tpu_custom_call" | custom-call | tf_op jit(solution)/shard_map/pallas_call | solution.py:604

commit v3 on v2

--- a/solution.py
+++ b/solution.py
@@ -8,12 +8,12 @@
 from jax.experimental.pallas import tpu as pltpu
 from jax.sharding import PartitionSpec as P
 
-DEEP_IN = 0.3
-DEEP_OUT = 0.2
+DEEP = 0.2
+EXTRA = 1
 TILE = 16
 SIDE = 2
 LATE = 2
-KINDS = 18
+KINDS = 20
 LINE = 4
 
 
@@ -24,16 +24,30 @@
     owners, deltas, master, momentum, load_sem, first, passed, second, zin, zrecv,
     staged, near, far, last, onward, ztotal, cross,
     apack, arecv, mean, packed, slotted, squares, others,
-    send_sem, recv_sem,
+    send_sem, recv_sem, ready,
 ):
-    wa, wb, wc, ws = plan
+    wa, wb, wc, extra = plan
     pod_count, rep_count, shard_count = axis_sizes
     blocks, sub_rows, slots = deltas.shape[0], master.shape[1], master.shape[0]
     widths = (wa, wb, wc)
     base = (0, pod_count * wa, pod_count * (wa + wb))
     offset = (0, wa, wa + wb)
-    pair = (wa, ws)
-    pair_width, deep_width = wa + ws, wb - ws + wc
+
+    def pair(b):
+        return (wa, wb - extra if b < blocks // 2 else wb)
+
+    def pair_width(b):
+        return sum(pair(b))
+
+    def deep_width(b):
+        return wa + wb + wc - pair_width(b)
+
+    def part(r, b):
+        return pl.ds(0, pair(b)[r])
+
+    def deep(b):
+        return pl.ds(0, pod_count * deep_width(b))
+
     o, q, s = lax.axis_index("outer"), lax.axis_index("rep"), lax.axis_index("shard")
     y, x = o // SIDE, o % SIDE
     neighbour = {"x": y * SIDE + 1 - x, "y": (1 - y) * SIDE + x}
@@ -48,14 +62,17 @@
         return ((y + d // SIDE) % SIDE) * SIDE + (x + d % SIDE) % SIDE
 
     barrier = pltpu.get_barrier_semaphore()
-    peers = []
-    for d in range(pod_count):
-        for e in range(rep_count):
-            if d or e:
-                peers.append({"outer": pod(d), "rep": (q + e) % rep_count})
-    peers += [{"shard": (s + d) % shard_count} for d in range(1, shard_count)]
-    for peer in peers:
-        pl.semaphore_signal(barrier, inc=1, device_id=peer, device_id_type=pl.DeviceIdType.MESH)
+
+    def greet(sem, **to):
+        pl.semaphore_signal(sem, inc=1, device_id=to, device_id_type=pl.DeviceIdType.MESH)
+
+    middle = jnp.logical_not(is_tip)
+    greet(barrier, outer=neighbour["x"])
+    greet(barrier, outer=neighbour["y"])
+    greet(barrier, rep=jnp.where(is_tip, place(1), place(0)))
+    pl.when(middle)(lambda: greet(barrier, rep=place(2)))
+    for d in range(1, shard_count):
+        greet(barrier, shard=(s + d) % shard_count)
     loads = [
         pltpu.make_async_copy(deltas_far.at[b], deltas.at[b], load_sem.at[b]) for b in range(blocks)
     ]
@@ -64,13 +81,30 @@
     loads.append(pltpu.make_async_copy(owners_far, owners, load_sem.at[blocks + 2]))
     for load in loads:
         load.start()
-    pl.semaphore_wait(barrier, len(peers))
-
-    numbers, sent, roles = {}, {}, {}
+    pl.semaphore_wait(barrier, jnp.where(is_tip, 3, 4) + shard_count - 1)
+    pl.when(middle)(lambda: greet(ready, rep=place(2)))
+
+    def pass_ready():
+        @pl.when(middle)
+        def _():
+            pl.semaphore_wait(ready, 1)
+            greet(ready, rep=place(0))
+
+    def all_ready():
+        pl.when(is_tip)(lambda: pl.semaphore_wait(ready, 1))
+
+
+    sent, roles = {}, {}
+    spans, phases = (("slot", 0), ("slot", 1), ("early",), ("norm",), ("shard",)), ({}, {})
+    gathers = ("wide", "up", "over", "down", "outward", "across", "inward", "block", "blocks")
 
     def copy(group, src, dst, **to):
         kind = group[0]
-        number = numbers.setdefault(group, len(numbers))
+        if group in spans:
+            number = spans.index(group)
+        else:
+            numbers = phases[kind in gathers]
+            number = len(spans) + numbers.setdefault(group, len(numbers))
         sent.setdefault(kind, len(sent))
         return pltpu.make_async_remote_copy(
             src_ref=src, dst_ref=dst, send_sem=send_sem.at[sent[kind]], recv_sem=recv_sem.at[number],
@@ -115,17 +149,17 @@
         width = widths[region]
         return pl.ds(pl.multiple_of(base[region] + k * width, 128), width)
 
-    def pair_cols(r, k):
-        return pl.ds(pl.multiple_of(base[r] + k * widths[r], 128), pair[r])
+    def pair_cols(r, b, k):
+        return pl.ds(pl.multiple_of(base[r] + k * widths[r], 128), pair(b)[r])
 
     def local_cols(region):
         return pl.ds(offset[region], widths[region])
 
-    def pair_local(r):
-        return pl.ds(offset[r], pair[r])
-
-    def deep_cols(k):
-        return pl.ds(pl.multiple_of(k * deep_width, 128), deep_width)
+    def pair_local(r, b):
+        return pl.ds(offset[r], pair(b)[r])
+
+    def deep_cols(b, k):
+        return pl.ds(pl.multiple_of(k * deep_width(b), 128), deep_width(b))
 
     def order(region, b):
         return ("x", "y") if (region + b) % 2 == 0 else ("y", "x")
@@ -161,87 +195,102 @@
             axis = order(r, b)[0]
             for j in range(SIDE):
                 send(
-                    ("first", b, g), deltas.at[b, i, :, pair_cols(r, quarter(axis, j, True))],
-                    first[r].at[j, b, i], outer=neighbour[axis],
+                    ("first", b, g), deltas.at[b, i, :, pair_cols(r, b, quarter(axis, j, True))],
+                    first[r].at[j, b, i, :, part(r, b)], outer=neighbour[axis],
                 )
 
     def send_second(b, g):
-        arrive(("first", b, g), deltas.at[b, at_rows(g), :, pl.ds(0, SIDE * pair_width)])
+        arrive(("first", b, g), deltas.at[b, at_rows(g), :, pl.ds(0, SIDE * pair_width(b))])
         for r in range(2):
             axis, other = order(r, b)
             go = 1 - stay(axis)
-            at = pair_cols(r, quarter(axis, go, False))
+            at = pair_cols(r, b, quarter(axis, go, False))
 
             def body(i):
-                passed[r][b, i] = down(up(deltas[b, i, :, at]) + up(first[r][go, b, i]))
+                came = first[r][go, b, i, :, part(r, b)]
+                passed[r][b, i, :, part(r, b)] = down(up(deltas[b, i, :, at]) + up(came))
 
             each(g, body)
             i = at_rows(g)
-            send(("second", b, g), passed[r].at[b, i], second[r].at[b, i], outer=neighbour[other])
+            send(
+                ("second", b, g), passed[r].at[b, i, :, part(r, b)],
+                second[r].at[b, i, :, part(r, b)], outer=neighbour[other],
+            )
 
     def pair_total(r, b, i):
-        total = up(deltas[b, i, :, pair_cols(r, o)]) + up(first[r][stay(order(r, b)[0]), b, i])
-        return total + up(second[r][b, i])
+        at = part(r, b)
+        total = up(deltas[b, i, :, pair_cols(r, b, o)]) + up(first[r][stay(order(r, b)[0]), b, i, :, at])
+        return total + up(second[r][b, i, :, at])
 
     def send_third(b):
         groups = others_of if late(b) else tail
         for g in groups:
-            arrive(("second", b, g), deltas.at[b, at_rows(g), :, pl.ds(0, pair_width)])
+            arrive(("second", b, g), deltas.at[b, at_rows(g), :, pl.ds(0, pair_width(b))])
         for d in others_of:
             there = (q + d) % rep_count
             for r in range(2):
-                zin[b, d - 1, :, pair_local(r)] = down(pair_total(r, b, there))
-            send(("third", b), zin.at[b, d - 1], zrecv.at[d - 1, b], rep=there)
+                zin[b, d - 1, :, pair_local(r, b)] = down(pair_total(r, b, there))
+            at = pl.ds(0, pair_width(b))
+            send(("third", b), zin.at[b, d - 1, :, at], zrecv.at[d - 1, b, :, at], rep=there)
 
     def deep_of(b, i):
+        keep = pair(b)[1]
+        if keep == wb:
+            return deltas[b, i, :, whole]
         parts = []
         for k in range(pod_count):
-            parts.append(deltas[b, i, :, pl.ds(base[1] + k * wb + ws, wb - ws)])
+            parts.append(deltas[b, i, :, pl.ds(base[1] + k * wb + keep, wb - keep)])
             parts.append(deltas[b, i, :, pl.ds(base[2] + k * wc, wc)])
-        return jnp.concatenate([p for p in parts if p.shape[-1]], axis=-1)
+        return jnp.concatenate(parts, axis=-1)
 
     def start_tips(b):
         @pl.when(is_tip)
         def _():
             for k in (3, 2, 1):
-                staged[k - 1, b] = deep_of(b, place(k))
-                copy(("near", b, k), staged.at[k - 1, b], near.at[k - 1, b], rep=place(1)).start()
+                staged[k - 1, b, :, deep(b)] = deep_of(b, place(k))
+                copy(("near", b, k), staged.at[k - 1, b, :, deep(b)], near.at[k - 1, b, :, deep(b)], rep=place(1)).start()
 
         roles["near"] = is_tip
 
     def relay_near(b):
-        @pl.when(jnp.logical_not(is_tip))
+        @pl.when(middle)
         def _():
             for k in (3, 2):
-                arrive(("near", b, k), near.at[k - 1, b])
-                onward[k - 1, b] = down(up(deep_of(b, place(k))) + up(near[k - 1, b]))
-                copy(("far", b, 3 - k), onward.at[k - 1, b], far.at[3 - k, b], rep=place(2)).start()
-
-        roles["far"] = jnp.logical_not(is_tip)
+                arrive(("near", b, k), near.at[k - 1, b, :, deep(b)])
+                onward[k - 1, b, :, deep(b)] = down(up(deep_of(b, place(k))) + up(near[k - 1, b, :, deep(b)]))
+                copy(("far", b, 3 - k), onward.at[k - 1, b, :, deep(b)], far.at[3 - k, b, :, deep(b)], rep=place(2)).start()
+
+        roles["far"] = middle
 
     def relay_far(b):
-        @pl.when(jnp.logical_not(is_tip))
+        @pl.when(middle)
         def _():
-            arrive(("far", b, 0), far.at[0, b])
-            onward[0, b] = down(up(deep_of(b, place(0))) + up(far[0, b]))
-            copy(("last", b), onward.at[0, b], last.at[b], rep=place(0)).start()
-
-        roles["last"] = jnp.logical_not(is_tip)
+            arrive(("far", b, 0), far.at[0, b, :, deep(b)])
+            onward[0, b, :, deep(b)] = down(up(deep_of(b, place(0))) + up(far[0, b, :, deep(b)]))
+            copy(("last", b), onward.at[0, b, :, deep(b)], last.at[b, :, deep(b)], rep=place(0)).start()
+
+        roles["last"] = middle
 
     def send_cross(b):
+        at = deep(b)
+
         @pl.when(is_tip)
         def _():
-            arrive(("last", b), last.at[b])
-            ztotal[b] = down(up(deep_of(b, q)) + up(last[b]))
-
-        @pl.when(jnp.logical_not(is_tip))
+            arrive(("last", b), last.at[b, :, at])
+            ztotal[b, :, at] = down(up(deep_of(b, q)) + up(last[b, :, at]))
+
+        @pl.when(middle)
         def _():
-            arrive(("near", b, 1), near.at[0, b])
-            arrive(("far", b, 1), far.at[1, b])
-            ztotal[b] = down(up(deep_of(b, q)) + up(near[0, b]) + up(far[1, b]))
+            arrive(("near", b, 1), near.at[0, b, :, at])
+            arrive(("far", b, 1), far.at[1, b, :, at])
+            total = up(deep_of(b, q)) + up(near[0, b, :, at])
+            ztotal[b, :, at] = down(total + up(far[1, b, :, at]))
 
         for d in range(1, pod_count):
-            send(("cross", b), ztotal.at[b, :, deep_cols(pod(d))], cross.at[d - 1, b], outer=pod(d))
+            send(
+                ("cross", b), ztotal.at[b, :, deep_cols(b, pod(d))],
+                cross.at[d - 1, b, :, pl.ds(0, deep_width(b))], outer=pod(d),
+            )
 
     scale = 1.0 / (pod_count * rep_count)
 
@@ -258,20 +307,21 @@
 
     def finish_pair(b):
         if late(b):
-            arrive(("second", b, 0), deltas.at[b, q, :, pl.ds(0, pair_width)])
-        arrive(("third", b), zrecv.at[:, b])
+            arrive(("second", b, 0), deltas.at[b, q, :, pl.ds(0, pair_width(b))])
+        arrive(("third", b), zrecv.at[:, b, :, pl.ds(0, pair_width(b))])
         for r in range(2):
             total = pair_total(r, b, q)
             for d in range(rep_count - 1):
-                total = total + up(zrecv[d, b, :, pair_local(r)])
-            put_mean(b, pair_local(r), total)
+                total = total + up(zrecv[d, b, :, pair_local(r, b)])
+            put_mean(b, pair_local(r, b), total)
 
     def finish_cross(b):
-        arrive(("cross", b), cross.at[:, b])
-        total = up(ztotal[b, :, deep_cols(o)])
+        at = pl.ds(0, deep_width(b))
+        arrive(("cross", b), cross.at[:, b, :, at])
+        total = up(ztotal[b, :, deep_cols(b, o)])
         for d in range(pod_count - 1):
-            total = total + up(cross[d, b])
-        put_mean(b, pl.ds(pair_width, deep_width), total)
+            total = total + up(cross[d, b, :, at])
+        put_mean(b, pl.ds(pair_width(b), deep_width(b)), total)
 
     owner, rank = [], []
 
@@ -324,15 +374,15 @@
                         outer=pod(d), rep=(q + e) % rep_count,
                     )
 
-    def mean_send():
+    def mean_send(part):
+        at = pl.ds(wa + wb, wc) if part == 0 else pl.ds(0, wa + wb)
         for d in range(pod_count):
             for j in range(slots):
-                index = block_of(pod(d), j)[0]
-                packed[d, j] = mean[index]
+                packed[d, j, :, at] = mean[block_of(pod(d), j)[0], :, at]
             if d == 0:
-                slotted[o] = packed[0]
+                slotted[o, :, :, at] = packed[0, :, :, at]
             else:
-                send(("slot",), packed.at[d], slotted.at[o], outer=pod(d))
+                send(("slot", part), packed.at[d, :, :, at], slotted.at[o, :, :, at], outer=pod(d))
 
     def norm_wait():
         arrive(("norm",), others.at[pl.ds(1, group - 1)])
@@ -364,32 +414,44 @@
             at = out.at[b, q, :, cols(2, o)]
             send(("wide", b), at, at, outer=pod(d))
 
+    def pass_line(role, group, b, k, **to):
+        for r in range(2):
+            at = out.at[b, place(k), :, cols(r, o)]
+            send_if(role, group, at, at, **to)
+
+    def line_rows(b, count):
+        return out.at[b, pl.ds(0, count), :, pl.ds(0, wa + wb)]
+
     def send_line(b):
-        for d in others_of:
-            for r in range(2):
-                at = out.at[b, q, :, cols(r, o)]
-                send(("line", b, d), at, at, rep=(q + d) % rep_count)
-
-    middle = jnp.logical_not(is_tip)
+        pass_line(is_tip, ("up", b), b, 0, rep=place(1))
+        pass_line(middle, ("down", b), b, 1, rep=place(0))
+        pass_line(middle, ("over", b, 1), b, 1, rep=place(2))
+
+    def line_near(b):
+        pl.when(middle)(lambda: arrive(("over", b, 1), line_rows(b, 1)))
+        pass_line(middle, ("down", b), b, 2, rep=place(0))
+        pl.when(middle)(lambda: arrive(("up", b), line_rows(b, 1)))
+        pass_line(middle, ("over", b, 0), b, 0, rep=place(2))
+
+    def line_far(b):
+        pl.when(middle)(lambda: arrive(("over", b, 0), line_rows(b, 1)))
+        pass_line(middle, ("down", b), b, 3, rep=place(0))
 
     def line(b):
         arrive(("wide", b), out.at[b, q, :, pl.ds(0, (pod_count - 1) * wc)])
         mine = out.at[b, q, :, whole]
         send_if(is_tip, ("outward", b, 0), mine, mine, rep=place(1))
         send_if(middle, ("across", b, 1), mine, mine, rep=place(2))
-        send_if(middle, ("inward",), mine, mine, rep=place(0))
 
     def line_across(b):
         at = out.at[b, place(0), :, whole]
         pl.when(middle)(lambda: arrive(("outward", b, 0), at))
         send_if(middle, ("across", b, 0), at, at, rep=place(2))
-        at2 = out.at[b, place(2), :, whole]
-        pl.when(middle)(lambda: arrive(("across", b, 1), at2))
-        send_if(middle, ("inward",), at2, at2, rep=place(0))
-
-    def line_inward(b):
-        at = out.at[b, place(3), :, whole]
-        pl.when(middle)(lambda: arrive(("across", b, 0), at))
+
+    def line_inward(b, k):
+        at = out.at[b, place(k), :, whole]
+        if k > 1:
+            pl.when(middle)(lambda: arrive(("across", b, 3 - k), at))
         send_if(middle, ("inward",), at, at, rep=place(0))
 
     def line_end():
@@ -397,8 +459,6 @@
 
     def send_block(b, d):
         i = (q + rep_count - d) % rep_count
-        if d:
-            arrive(("line", b, d), out.at[b, i, :, pl.ds(0, wa + wb)])
         for r in range(2):
             at = out.at[b, i, :, cols(r, o)]
             send(("block", b, d), at, at, outer=neighbour[order(r, b)[1]])
@@ -413,7 +473,8 @@
                 send(("blocks",), at, at, outer=neighbour[axis])
 
     def update(factor):
-        arrive(("slot",), slotted.at[pl.ds(1, pod_count - 1)])
+        for part, width in enumerate((wc, wa + wb)):
+            arrive(("slot", part), slotted.at[pl.ds(1, pod_count - 1), :, :, pl.ds(0, width)])
         for j in range(slots):
             found = block_of(o, j)[1].astype(jnp.float32)
             for k in range(pod_count):
@@ -428,24 +489,42 @@
         arrive(("blocks",), out.at[:, :, :, pl.ds(0, SIDE * (wa + wb))])
 
     def drain():
-        leave("first", deltas.at[:, :, :, pl.ds(0, SIDE * pair_width)])
-        leave("second", deltas.at[:, :, :, pl.ds(0, pair_width)])
-        leave("third", zin)
-        leave("near", staged)
-        leave("far", far)
-        leave("last", last)
-        leave("cross", cross)
+        pairs = sum(pair_width(b) for b in range(blocks))
+        deeps = sum(deep_width(b) for b in range(blocks))
+        some = blocks // 2
+
+        def rows(count, width):
+            return deltas.at[0, pl.ds(0, count), :, pl.ds(0, width)]
+
+        leave("first", deltas.at[pl.ds(0, some), :, :, pl.ds(0, SIDE * pairs // some)])
+        leave("second", deltas.at[pl.ds(0, some), :, :, pl.ds(0, pairs // some)])
+        leave("third", rows(rep_count - 1, pairs))
+        leave("near", rows(3, pod_count * deeps))
+        leave("far", rows(2, pod_count * deeps))
+        leave("last", rows(1, pod_count * deeps))
+        leave("cross", rows(pod_count - 1, deeps))
         leave("early", arecv.at[pl.ds(1, pod_count - 1)])
         leave("norm", others.at[pl.ds(1, group - 1)])
         leave("slot", slotted.at[pl.ds(1, pod_count - 1)])
         leave("shard", others.at[pl.ds(group + 1, shard_count - 1)])
         leave("wide", out.at[:, 0, :, pl.ds(0, (pod_count - 1) * wc)])
-        leave("line", out.at[:, pl.ds(0, rep_count - 1), :, pl.ds(0, wa + wb)])
+        leave("up", out.at[:, 0, :, pl.ds(0, wa + wb)])
+        leave("over", out.at[:, pl.ds(0, 2), :, pl.ds(0, wa + wb)])
+        leave("down", out.at[:, pl.ds(0, 3), :, pl.ds(0, wa + wb)])
         leave("outward", out.at[:, 0, :, whole])
         leave("across", out.at[:, pl.ds(0, 2), :, whole])
         leave("inward", out.at[:, pl.ds(0, 3), :, whole])
         leave("block", out.at[:, :, :, pl.ds(0, wa + wb)])
         leave("blocks", out.at[:, :, :, pl.ds(0, SIDE * (wa + wb))])
+
+    def rests(b):
+        pl.when(is_tip)(lambda: arrive(("down", b), line_rows(b, 3)))
+        for d in others_of:
+            send_block(b, d)
+
+    def rests_on(b):
+        for d in others_of:
+            send_blocks(b, d)
 
     squares[0] = jnp.zeros(squares.shape[1:], jnp.float32)
     def firsts(b):
@@ -468,7 +547,11 @@
     for t in range(blocks + 2):
         if t < blocks:
             relay_near(t)
+            if t == 0:
+                pass_ready()
             seconds(t)
+            if t == 0:
+                all_ready()
         if t + 2 < blocks:
             firsts(t + 2)
             if t + 3 == blocks:
@@ -487,43 +570,62 @@
         if 0 <= t - 2 < blocks:
             send_cross(t - 2)
     for b in range(blocks):
+        if b < 2:
+            finish_pair(b)
+        finish_cross(b)
+    mean_send(0)
+    for b in range(2, blocks):
         finish_pair(b)
-        finish_cross(b)
     norm_send()
-    mean_send()
+    mean_send(1)
     norm_wait()
     factor = norm_shard()
     for b in range(blocks):
         spread(b, factor)
         send_wide(b)
+        send_line(b)
         send_block(b, 0)
-        if b == 0:
-            send_line(0)
     for b in range(blocks):
         line(b)
-        for later in {0: (1,), 1: (2, 3)}.get(b, ()):
-            send_line(later)
+        send_blocks(b, 0)
+        line_near(b)
+    line_far(0)
+    rests(0)
+    line_far(1)
+    line_across(0)
+    rests(1)
+    rests_on(0)
+    line_far(2)
+    line_across(1)
+    rests(2)
+    line_far(3)
+    rests_on(1)
+    rests(3)
+    line_across(2)
+    line_across(3)
     for b in range(blocks):
-        send_blocks(b, 0)
-    for b in range(blocks):
-        for d in others_of:
-            send_block(b, d)
-        line_across(b)
-        for d in others_of:
-            send_blocks(b, d)
-        if b == 1:
-            update(factor)
-    for b in range(blocks):
-        line_inward(b)
+        line_inward(b, 1)
+        line_inward(b, 2)
+    rests_on(2)
+    update(factor)
+    line_inward(0, 3)
+    line_inward(1, 3)
+    rests_on(3)
+    line_inward(2, 3)
+    line_inward(3, 3)
     line_end()
     finish()
     drain()
-    assert len(numbers) == recv_sem.shape[0] and len(sent) == send_sem.shape[0]
+    assert len(spans) + max(len(p) for p in phases) == recv_sem.shape[0]
+    assert len(sent) == send_sem.shape[0]
 
 
 def store(*refs):
     sem = refs[-1]
-    copies = [pltpu.make_async_copy(refs[i], refs[i + 3], sem.at[i]) for i in range(3)]
+    copies = []
+    for i in range(3):
+        for k in range(refs[i].shape[0]):
+            copies.append(pltpu.make_async_copy(refs[i].at[k], refs[i + 3].at[k], sem.at[len(copies)]))
     for copy in copies:
         copy.start()
     for copy in copies:
@@ -532,10 +634,9 @@
 
 def regions(width, pod_count):
     tiles = width // (128 * pod_count)
-    deep = round(tiles * DEEP_IN)
-    wc = min(deep, round(tiles * DEEP_OUT))
+    wc = max(1, round(tiles * DEEP))
     wb = (tiles - wc) // 2
-    return tuple(128 * n for n in (tiles - wc - wb, wb, wc, wb - (deep - wc)))
+    return tuple(128 * n for n in (tiles - wc - wb, wb, wc, EXTRA))
 
 
 def fused(deltas, owners, master, momentum):
@@ -546,11 +647,12 @@
     entries = shard_count * blocks * rep_count * sub_rows * width
     clip_limit = 0.5 * math.sqrt(entries)
     widths = regions(width, pod_count)
-    wa, wb, wc, ws = widths
-    part, deep_width = width // pod_count, wb - ws + wc
+    wa, wb, wc, extra = widths
+    part, deep_width = width // pod_count, extra + wc
     deep = pod_count * deep_width
     group = pod_count * rep_count
-    waits = 2 * (blocks + (rep_count - 1) * LATE) + 8 * blocks + 4 + blocks * (2 * rep_count + 3) + 2
+    reduce_waits = 2 * (blocks + (rep_count - 1) * LATE) + 8 * blocks
+    waits = 5 + max(reduce_waits, blocks * (rep_count + 8) + 2)
     vmem, hbm = pl.BlockSpec(memory_space=pltpu.VMEM), pl.BlockSpec(memory_space=pltpu.HBM)
     bf16, f32 = jnp.bfloat16, jnp.float32
     V = pltpu.VMEM
@@ -569,11 +671,11 @@
             V(master.shape[2:], f32),
             V(master.shape[2:], f32),
             pltpu.SemaphoreType.DMA((blocks + 3,)),
-            [V((SIDE, blocks, rep_count, sub_rows, w), bf16) for w in (wa, ws)],
-            [V((blocks, rep_count, sub_rows, w), bf16) for w in (wa, ws)],
-            [V((blocks, rep_count, sub_rows, w), bf16) for w in (wa, ws)],
-            V((blocks, rep_count - 1, sub_rows, wa + ws), bf16),
-            V((rep_count - 1, blocks, sub_rows, wa + ws), bf16),
+            [V((SIDE, blocks, rep_count, sub_rows, w), bf16) for w in (wa, wb)],
+            [V((blocks, rep_count, sub_rows, w), bf16) for w in (wa, wb)],
+            [V((blocks, rep_count, sub_rows, w), bf16) for w in (wa, wb)],
+            V((blocks, rep_count - 1, sub_rows, wa + wb), bf16),
+            V((rep_count - 1, blocks, sub_rows, wa + wb), bf16),
             V((3, blocks, sub_rows, deep), bf16),
             V((3, blocks, sub_rows, deep), bf16),
             V((2, blocks, sub_rows, deep), bf16),
@@ -590,6 +692,7 @@
             V((group + shard_count, 1, 128), f32),
             pltpu.SemaphoreType.DMA((KINDS,)),
             pltpu.SemaphoreType.DMA((waits,)),
+            pltpu.SemaphoreType.REGULAR,
         ],
         compiler_params=pltpu.CompilerParams(
             collective_id=0, has_side_effects=True, vmem_limit_bytes=48 * 1024 * 1024
@@ -606,7 +709,7 @@
         out_shape=tuple(jax.ShapeDtypeStruct(a.shape, a.dtype) for a in arrays),
         in_specs=[pl.BlockSpec(memory_space=pl.ANY)] * 3,
         out_specs=(hbm,) * 3,
-        scratch_shapes=[pltpu.SemaphoreType.DMA((3,))],
+        scratch_shapes=[pltpu.SemaphoreType.DMA((blocks + 2 * slots,))],
         compiler_params=pltpu.CompilerParams(vmem_limit_bytes=4 * 1024 * 1024),
     )(*(pltpu.with_memory_space_constraint(a, pltpu.VMEM) for a in arrays))
     return (
@@ -670,6 +773,9 @@
         tiled = width % (SIDE * SIDE * 128) == 0 and width >= 3 * SIDE * SIDE * 128
         tiled = tiled and sub_rows % TILE == 0 and blocks == SIDE * SIDE
         tiled = tiled and deltas.shape[2] == blocks * LINE * sub_rows
+        if tiled:
+            wa, wb, wc, extra = regions(width, SIDE * SIDE)
+            tiled = wb > extra and SIDE * SIDE * blocks * (wc + extra // 2) <= width
         return (fused if fits and tiled else local)(deltas, owners, master, momentum)
 
     return jax.shard_map(

time: 104 us -> 101 us (0.971)
  Pallas kernels: 103 us -> 100 us
    pallas_call x1, Pallas kernels: 100 us -> 96.9 us  [fused(): pl.pallas_call(functools.partial(kernel, widths, (pod_count, rep_count, s...]
where the time goes in v3:
time: 101 us
  Pallas kernels  100 us (99%)
    pallas_call x1, Pallas kernels, fused(): pl.pallas_call(functools.partial(kernel, widths, (pod_count, rep_count, s...  96.9 us
    pallas_call x1, Pallas kernels, fused(): pl.pallas_call(store, out_shape=tuple((jax.ShapeDtypeStruct(a.shape, a.dt...  3.23 us

profile of v3, /device:TPU:0, one launch (start us, length us, event | category | flops | bytes accessed | tf_op | source)
XLA Modules:
  0.0 100.8 jit_solution(16206878899845025908)
XLA Ops:
  0.6 96.9 %shard_map.67 = (bf16[4,4,32,5120]{3,2,1,0:T(8,128)(2,1)S(1)}, f32[2,32,5120]{2,1,0:T(8,128)S(1)}, f32[2,32,5120]{2,1,0:T(8,128)S(1)}) custom-call(s32[4]{0:T(128)} %bitcast.10, bf16[4,4,32,5120]{3,2,1,0:T(8,128)(2,1)} %bitcast.7, f32[2,32,5120]{2,1,0:T(8,128)} %bitcast.8, f32[2,32,5120]{2,1,0:T(8,128)} %bitcast.9), custom_call_target="tpu_custom_call" | custom-call | tf_op jit(solution)/shard_map/pallas_call | solution.py:659
  97.6 3.2 %shard_map.68 = (bf16[4,4,32,5120]{3,2,1,0:T(8,128)(2,1)}, f32[2,32,5120]{2,1,0:T(8,128)}, f32[2,32,5120]{2,1,0:T(8,128)}) custom-call(bf16[4,4,32,5120]{3,2,1,0:T(8,128)(2,1)S(1)} %get-tuple-element.9.refs_0_, f32[2,32,5120]{2,1,0:T(8,128)S(1)} %get-tuple-element.10.refs_1_, f32[2,32,5120]{2,1,0:T(8,128)S(1)} %get-tuple-element.11.refs_2_), custom_call_target="tpu_custom_call" | custom-call | tf_op jit(solution)/shard_map/pallas_call | solution.py:707

commit v4 on v3

--- a/solution.py
+++ b/solution.py
@@ -10,6 +10,7 @@
 
 DEEP = 0.2
 EXTRA = 1
+THICK = 2
 TILE = 16
 SIDE = 2
 LATE = 2
@@ -34,7 +35,7 @@
     offset = (0, wa, wa + wb)
 
     def pair(b):
-        return (wa, wb - extra if b < blocks // 2 else wb)
+        return (wa, wb - extra if b < THICK else wb)
 
     def pair_width(b):
         return sum(pair(b))
@@ -422,8 +423,10 @@
     def line_rows(b, count):
         return out.at[b, pl.ds(0, count), :, pl.ds(0, wa + wb)]
 
-    def send_line(b):
+    def send_up(b):
         pass_line(is_tip, ("up", b), b, 0, rep=place(1))
+
+    def send_mid(b):
         pass_line(middle, ("down", b), b, 1, rep=place(0))
         pass_line(middle, ("over", b, 1), b, 1, rep=place(2))
 
@@ -437,10 +440,17 @@
         pl.when(middle)(lambda: arrive(("over", b, 0), line_rows(b, 1)))
         pass_line(middle, ("down", b), b, 3, rep=place(0))
 
-    def line(b):
+    def wide_done(b):
         arrive(("wide", b), out.at[b, q, :, pl.ds(0, (pod_count - 1) * wc)])
+
+    def line_tip(b):
         mine = out.at[b, q, :, whole]
+        pl.when(is_tip)(lambda: wide_done(b))
         send_if(is_tip, ("outward", b, 0), mine, mine, rep=place(1))
+
+    def line_mid(b):
+        mine = out.at[b, q, :, whole]
+        pl.when(middle)(lambda: wide_done(b))
         send_if(middle, ("across", b, 1), mine, mine, rep=place(2))
 
     def line_across(b):
@@ -496,12 +506,15 @@
         def rows(count, width):
             return deltas.at[0, pl.ds(0, count), :, pl.ds(0, width)]
 
-        leave("first", deltas.at[pl.ds(0, some), :, :, pl.ds(0, SIDE * pairs // some)])
-        leave("second", deltas.at[pl.ds(0, some), :, :, pl.ds(0, pairs // some)])
+        def deep_rows(count):
+            return deltas.at[pl.ds(0, some), pl.ds(0, count), :, pl.ds(0, pod_count * deeps // some)]
+
+        leave("first", deltas.at[pl.ds(0, SIDE), :, :, pl.ds(0, pairs)])
+        leave("second", rows(rep_count, pairs))
         leave("third", rows(rep_count - 1, pairs))
-        leave("near", rows(3, pod_count * deeps))
-        leave("far", rows(2, pod_count * deeps))
-        leave("last", rows(1, pod_count * deeps))
+        leave("near", deep_rows(3))
+        leave("far", deep_rows(2))
+        leave("last", deep_rows(1))
         leave("cross", rows(pod_count - 1, deeps))
         leave("early", arecv.at[pl.ds(1, pod_count - 1)])
         leave("norm", others.at[pl.ds(1, group - 1)])
@@ -583,22 +596,38 @@
     for b in range(blocks):
         spread(b, factor)
         send_wide(b)
-        send_line(b)
+        send_up(b)
+        if b < 2:
+            send_mid(b)
         send_block(b, 0)
-    for b in range(blocks):
-        line(b)
-        send_blocks(b, 0)
-        line_near(b)
+    line_near(0)
+    send_blocks(0, 0)
+    line_tip(0)
+    line_near(1)
+    send_blocks(1, 0)
+    line_tip(1)
+    send_mid(2)
     line_far(0)
+    send_blocks(2, 0)
+    send_blocks(3, 0)
+    line_tip(2)
+    line_tip(3)
     rests(0)
+    line_near(2)
     line_far(1)
+    send_mid(3)
+    line_near(3)
+    rests(1)
+    line_mid(0)
+    line_mid(1)
+    line_far(2)
+    line_mid(2)
+    line_mid(3)
+    rests_on(0)
     line_across(0)
-    rests(1)
-    rests_on(0)
-    line_far(2)
-    line_across(1)
     rests(2)
     line_far(3)
+    line_across(1)
     rests_on(1)
     rests(3)
     line_across(2)
@@ -775,7 +804,7 @@
         tiled = tiled and deltas.shape[2] == blocks * LINE * sub_rows
         if tiled:
             wa, wb, wc, extra = regions(width, SIDE * SIDE)
-            tiled = wb > extra and SIDE * SIDE * blocks * (wc + extra // 2) <= width
+            tiled = wb > extra and SIDE * blocks * (wc + extra) <= width
         return (fused if fits and tiled else local)(deltas, owners, master, momentum)
 
     return jax.shard_map(

time: 101 us -> 99.2 us (0.982)
  Pallas kernels: 100 us -> 98.4 us
    pallas_call x1, Pallas kernels: 96.9 us -> 95.1 us  [fused(): pl.pallas_call(functools.partial(kernel, widths, (pod_count, rep_count, s...]
where the time goes in v4:
time: 99.2 us; the launch traced here: 99 us
  Pallas kernels  98.4 us (99%)
    pallas_call x1, Pallas kernels, fused(): pl.pallas_call(functools.partial(kernel, widths, (pod_count, rep_count, s...  95.1 us
    pallas_call x1, Pallas kernels, fused(): pl.pallas_call(store, out_shape=tuple((jax.ShapeDtypeStruct(a.shape, a.dt...  3.23 us

profile of v4, /device:TPU:0, one launch (start us, length us, event | category | flops | bytes accessed | tf_op | source)
XLA Modules:
  0.0 99.0 jit_solution(2686022359446602112)
XLA Ops:
  0.6 95.1 %shard_map.67 = (bf16[4,4,32,5120]{3,2,1,0:T(8,128)(2,1)S(1)}, f32[2,32,5120]{2,1,0:T(8,128)S(1)}, f32[2,32,5120]{2,1,0:T(8,128)S(1)}) custom-call(s32[4]{0:T(128)} %bitcast.10, bf16[4,4,32,5120]{3,2,1,0:T(8,128)(2,1)} %bitcast.7, f32[2,32,5120]{2,1,0:T(8,128)} %bitcast.8, f32[2,32,5120]{2,1,0:T(8,128)} %bitcast.9), custom_call_target="tpu_custom_call" | custom-call | tf_op jit(solution)/shard_map/pallas_call | solution.py:688
  95.8 3.2 %shard_map.68 = (bf16[4,4,32,5120]{3,2,1,0:T(8,128)(2,1)}, f32[2,32,5120]{2,1,0:T(8,128)}, f32[2,32,5120]{2,1,0:T(8,128)}) custom-call(bf16[4,4,32,5120]{3,2,1,0:T(8,128)(2,1)S(1)} %get-tuple-element.9.refs_0_, f32[2,32,5120]{2,1,0:T(8,128)S(1)} %get-tuple-element.10.refs_1_, f32[2,32,5120]{2,1,0:T(8,128)S(1)} %get-tuple-element.11.refs_2_), custom_call_target="tpu_custom_call" | custom-call | tf_op jit(solution)/shard_map/pallas_call | solution.py:736

commit v5 on v4

--- a/solution.py
+++ b/solution.py
@@ -14,7 +14,7 @@
 TILE = 16
 SIDE = 2
 LATE = 2
-KINDS = 20
+KINDS = 21
 LINE = 4
 
 
@@ -97,7 +97,7 @@
 
     sent, roles = {}, {}
     spans, phases = (("slot", 0), ("slot", 1), ("early",), ("norm",), ("shard",)), ({}, {})
-    gathers = ("wide", "up", "over", "down", "outward", "across", "inward", "block", "blocks")
+    gathers = ("wide", "wider", "up", "over", "down", "outward", "across", "inward", "block", "blocks")
 
     def copy(group, src, dst, **to):
         kind = group[0]
@@ -359,21 +359,39 @@
                 loop(slots, body)
         arecv[o] = apack[o]
 
-    def send_early():
-        for d in range(1, pod_count):
+    def send_early(*steps):
+        for d in steps:
             send(("early",), apack.at[pod(d)], arecv.at[o], outer=pod(d))
 
     group = pod_count * rep_count
 
+    lead = s == 0
+    follow = jnp.logical_not(lead)
+    partial = group + shard_count
+
     def norm_send():
-        others[0] = jnp.sum(squares[0], axis=0, keepdims=True)
-        for d in range(pod_count):
+        others[partial] = jnp.sum(squares[0], axis=0, keepdims=True)
+        send_if(follow, ("shard",), others.at[partial], others.at[group + s], shard=0)
+
+    def norm_lead():
+        roles["norm"] = lead
+
+        @pl.when(lead)
+        def _():
+            arrive(("shard",), others.at[pl.ds(group + 1, shard_count - 1)])
+            total = others[partial]
+            for d in range(1, shard_count):
+                total = total + others[group + d]
+            others[group] = total
+            others[0] = total
             for e in range(rep_count):
-                if d or e:
-                    send(
-                        ("norm",), others.at[0], others.at[d * rep_count + e],
-                        outer=pod(d), rep=(q + e) % rep_count,
-                    )
+                for d in range(pod_count):
+                    for t in range(shard_count):
+                        if d or e or t:
+                            copy(
+                                ("norm",), others.at[group], others.at[d * rep_count + e],
+                                outer=pod(d), rep=(q + e) % rep_count, shard=t,
+                            ).start()
 
     def mean_send(part):
         at = pl.ds(wa + wb, wc) if part == 0 else pl.ds(0, wa + wb)
@@ -386,20 +404,12 @@
                 send(("slot", part), packed.at[d, :, :, at], slotted.at[o, :, :, at], outer=pod(d))
 
     def norm_wait():
-        arrive(("norm",), others.at[pl.ds(1, group - 1)])
+        pl.when(lead)(lambda: arrive(("norm",), others.at[pl.ds(1, group - 1)]))
+        pl.when(follow)(lambda: arrive(("norm",), others.at[pl.ds(0, group)]))
+        arrive(("early",), arecv.at[pl.ds(1, pod_count - 1)])
         total = others[0]
         for d in range(1, group):
             total = total + others[d]
-        others[group] = total
-        for d in range(1, shard_count):
-            send(("shard",), others.at[group], others.at[group + d], shard=(s + d) % shard_count)
-        arrive(("early",), arecv.at[pl.ds(1, pod_count - 1)])
-
-    def norm_shard():
-        arrive(("shard",), others.at[pl.ds(group + 1, shard_count - 1)])
-        total = others[group]
-        for d in range(1, shard_count):
-            total = total + others[group + d]
         total = jnp.sum(total, keepdims=True)
         return jnp.minimum(1.0, clip_limit / jnp.sqrt(total + 1e-06))
 
@@ -411,9 +421,15 @@
             out[b, q, :, cols(r, o)] = down(value)
 
     def send_wide(b):
-        for d in range(1, pod_count):
-            at = out.at[b, q, :, cols(2, o)]
-            send(("wide", b), at, at, outer=pod(d))
+        at = out.at[b, q, :, cols(2, o)]
+        send(("wide", b), at, at, outer=neighbour[order(0, b)[0]])
+
+    def send_wider(b):
+        arrive(("wide", b), out.at[b, q, :, pl.ds(0, wc)])
+        axis, other = order(0, b)
+        for k in (o, neighbour[axis]):
+            at = out.at[b, q, :, cols(2, k)]
+            send(("wider", b), at, at, outer=neighbour[other])
 
     def pass_line(role, group, b, k, **to):
         for r in range(2):
@@ -441,7 +457,7 @@
         pass_line(middle, ("down", b), b, 3, rep=place(0))
 
     def wide_done(b):
-        arrive(("wide", b), out.at[b, q, :, pl.ds(0, (pod_count - 1) * wc)])
+        arrive(("wider", b), out.at[b, q, :, pl.ds(0, SIDE * wc)])
 
     def line_tip(b):
         mine = out.at[b, q, :, whole]
@@ -517,10 +533,11 @@
         leave("last", deep_rows(1))
         leave("cross", rows(pod_count - 1, deeps))
         leave("early", arecv.at[pl.ds(1, pod_count - 1)])
-        leave("norm", others.at[pl.ds(1, group - 1)])
+        leave("norm", others.at[pl.ds(0, group * shard_count - 1)])
         leave("slot", slotted.at[pl.ds(1, pod_count - 1)])
-        leave("shard", others.at[pl.ds(group + 1, shard_count - 1)])
-        leave("wide", out.at[:, 0, :, pl.ds(0, (pod_count - 1) * wc)])
+        leave("shard", others.at[pl.ds(0, 1)])
+        leave("wide", out.at[:, 0, :, pl.ds(0, wc)])
+        leave("wider", out.at[:, 0, :, pl.ds(0, SIDE * wc)])
         leave("up", out.at[:, 0, :, pl.ds(0, wa + wb)])
         leave("over", out.at[:, pl.ds(0, 2), :, pl.ds(0, wa + wb)])
         leave("down", out.at[:, pl.ds(0, 3), :, pl.ds(0, wa + wb)])
@@ -572,7 +589,7 @@
                     send_first(b, 0)
         if 0 <= t - 1 < blocks:
             if t == blocks:
-                send_early()
+                send_early(1, 2)
                 for b in range(blocks - LATE, blocks):
                     send_second(b, 0)
                 send_third(t - 1)
@@ -582,6 +599,7 @@
                 send_third(t - 1)
         if 0 <= t - 2 < blocks:
             send_cross(t - 2)
+    send_early(3)
     for b in range(blocks):
         if b < 2:
             finish_pair(b)
@@ -590,9 +608,9 @@
     for b in range(2, blocks):
         finish_pair(b)
     norm_send()
+    norm_lead()
     mean_send(1)
-    norm_wait()
-    factor = norm_shard()
+    factor = norm_wait()
     for b in range(blocks):
         spread(b, factor)
         send_wide(b)
@@ -601,17 +619,18 @@
             send_mid(b)
         send_block(b, 0)
     line_near(0)
+    send_wider(0)
     send_blocks(0, 0)
-    line_tip(0)
     line_near(1)
+    send_wider(1)
     send_blocks(1, 0)
-    line_tip(1)
     send_mid(2)
     line_far(0)
-    send_blocks(2, 0)
-    send_blocks(3, 0)
-    line_tip(2)
-    line_tip(3)
+    for b in range(2, blocks):
+        send_wider(b)
+        send_blocks(b, 0)
+    for b in range(blocks):
+        line_tip(b)
     rests(0)
     line_near(2)
     line_far(1)
@@ -681,7 +700,7 @@
     deep = pod_count * deep_width
     group = pod_count * rep_count
     reduce_waits = 2 * (blocks + (rep_count - 1) * LATE) + 8 * blocks
-    waits = 5 + max(reduce_waits, blocks * (rep_count + 8) + 2)
+    waits = 5 + max(reduce_waits, blocks * (rep_count + 9) + 2)
     vmem, hbm = pl.BlockSpec(memory_space=pltpu.VMEM), pl.BlockSpec(memory_space=pltpu.HBM)
     bf16, f32 = jnp.bfloat16, jnp.float32
     V = pltpu.VMEM
@@ -718,7 +737,7 @@
             V((pod_count, slots, sub_rows, part), bf16),
             V((pod_count, slots, sub_rows, part), bf16),
             V((1, 8, 128), f32),
-            V((group + shard_count, 1, 128), f32),
+            V((group * shard_count + shard_count, 1, 128), f32),
             pltpu.SemaphoreType.DMA((KINDS,)),
             pltpu.SemaphoreType.DMA((waits,)),
             pltpu.SemaphoreType.REGULAR,

time: 99.2 us -> 97.4 us (0.982)
  Pallas kernels: 98.4 us -> 96.6 us
    pallas_call x1, Pallas kernels: 95.1 us -> 93.4 us  [fused(): pl.pallas_call(functools.partial(kernel, widths, (pod_count, rep_count, s...]
where the time goes in v5:
time: 97.4 us; the launch traced here: 97.3 us
  Pallas kernels  96.6 us (99%)
    pallas_call x1, Pallas kernels, fused(): pl.pallas_call(functools.partial(kernel, widths, (pod_count, rep_count, s...  93.4 us
    pallas_call x1, Pallas kernels, fused(): pl.pallas_call(store, out_shape=tuple((jax.ShapeDtypeStruct(a.shape, a.dt...  3.23 us

profile of v5, /device:TPU:0, one launch (start us, length us, event | category | flops | bytes accessed | tf_op | source)
XLA Modules:
  0.0 97.3 jit_solution(1132469097471578129)
XLA Ops:
  0.6 93.4 %shard_map.67 = (bf16[4,4,32,5120]{3,2,1,0:T(8,128)(2,1)S(1)}, f32[2,32,5120]{2,1,0:T(8,128)S(1)}, f32[2,32,5120]{2,1,0:T(8,128)S(1)}) custom-call(s32[4]{0:T(128)} %bitcast.10, bf16[4,4,32,5120]{3,2,1,0:T(8,128)(2,1)} %bitcast.7, f32[2,32,5120]{2,1,0:T(8,128)} %bitcast.8, f32[2,32,5120]{2,1,0:T(8,128)} %bitcast.9), custom_call_target="tpu_custom_call" | custom-call | tf_op jit(solution)/shard_map/pallas_call | solution.py:707
  94.1 3.2 %shard_map.68 = (bf16[4,4,32,5120]{3,2,1,0:T(8,128)(2,1)}, f32[2,32,5120]{2,1,0:T(8,128)}, f32[2,32,5120]{2,1,0:T(8,128)}) custom-call(bf16[4,4,32,5120]{3,2,1,0:T(8,128)(2,1)S(1)} %get-tuple-element.9.refs_0_, f32[2,32,5120]{2,1,0:T(8,128)S(1)} %get-tuple-element.10.refs_1_, f32[2,32,5120]{2,1,0:T(8,128)S(1)} %get-tuple-element.11.refs_2_), custom_call_target="tpu_custom_call" | custom-call | tf_op jit(solution)/shard_map/pallas_call | solution.py:755

commit v6 on v5

--- a/solution.py
+++ b/solution.py
@@ -13,7 +13,7 @@
 THICK = 2
 TILE = 16
 SIDE = 2
-LATE = 2
+LATE = 4
 KINDS = 21
 LINE = 4
 
@@ -585,8 +585,11 @@
         if t + 2 < blocks:
             firsts(t + 2)
             if t + 3 == blocks:
-                for b in range(blocks - LATE, blocks):
+                for b in range(blocks - LATE, blocks - 2):
                     send_first(b, 0)
+        if t == blocks - 1:
+            for b in range(max(blocks - LATE, blocks - 2), blocks):
+                send_first(b, 0)
         if 0 <= t - 1 < blocks:
             if t == blocks:
                 send_early(1, 2)

time: 97.4 us -> 96.9 us (level)
  no operation moved by 1% of the time
where the time goes in v6:
time: 96.9 us; the launch traced here: 96.8 us
  Pallas kernels  96.1 us (99%)
    pallas_call x1, Pallas kernels, fused(): pl.pallas_call(functools.partial(kernel, widths, (pod_count, rep_count, s...  92.9 us
    pallas_call x1, Pallas kernels, fused(): pl.pallas_call(store, out_shape=tuple((jax.ShapeDtypeStruct(a.shape, a.dt...  3.23 us

profile of v6, /device:TPU:0, one launch (start us, length us, event | category | flops | bytes accessed | tf_op | source)
XLA Modules:
  0.0 96.8 jit_solution(16322499146124281507)
XLA Ops:
  0.6 92.9 %shard_map.67 = (bf16[4,4,32,5120]{3,2,1,0:T(8,128)(2,1)S(1)}, f32[2,32,5120]{2,1,0:T(8,128)S(1)}, f32[2,32,5120]{2,1,0:T(8,128)S(1)}) custom-call(s32[4]{0:T(128)} %bitcast.10, bf16[4,4,32,5120]{3,2,1,0:T(8,128)(2,1)} %bitcast.7, f32[2,32,5120]{2,1,0:T(8,128)} %bitcast.8, f32[2,32,5120]{2,1,0:T(8,128)} %bitcast.9), custom_call_target="tpu_custom_call" | custom-call | tf_op jit(solution)/shard_map/pallas_call | solution.py:710
  93.5 3.2 %shard_map.68 = (bf16[4,4,32,5120]{3,2,1,0:T(8,128)(2,1)}, f32[2,32,5120]{2,1,0:T(8,128)}, f32[2,32,5120]{2,1,0:T(8,128)}) custom-call(bf16[4,4,32,5120]{3,2,1,0:T(8,128)(2,1)S(1)} %get-tuple-element.9.refs_0_, f32[2,32,5120]{2,1,0:T(8,128)S(1)} %get-tuple-element.10.refs_1_, f32[2,32,5120]{2,1,0:T(8,128)S(1)} %get-tuple-element.11.refs_2_), custom_call_target="tpu_custom_call" | custom-call | tf_op jit(solution)/shard_map/pallas_call | solution.py:758

commit v7 on v6

--- a/solution.py
+++ b/solution.py
@@ -14,7 +14,7 @@
 TILE = 16
 SIDE = 2
 LATE = 4
-KINDS = 21
+KINDS = 14
 LINE = 4
 
 
@@ -96,15 +96,19 @@
 
 
     sent, roles = {}, {}
+    shared = {
+        "second": "first", "last": "far", "slot": "early", "outward": "up", "across": "over",
+        "inward": "down", "blocks": "block",
+    }
     spans, phases = (("slot", 0), ("slot", 1), ("early",), ("norm",), ("shard",)), ({}, {})
     gathers = ("wide", "wider", "up", "over", "down", "outward", "across", "inward", "block", "blocks")
 
     def copy(group, src, dst, **to):
-        kind = group[0]
+        kind = shared.get(group[0], group[0])
         if group in spans:
             number = spans.index(group)
         else:
-            numbers = phases[kind in gathers]
+            numbers = phases[group[0] in gathers]
             number = len(spans) + numbers.setdefault(group, len(numbers))
         sent.setdefault(kind, len(sent))
         return pltpu.make_async_remote_copy(
@@ -214,7 +218,7 @@
             each(g, body)
             i = at_rows(g)
             send(
-                ("second", b, g), passed[r].at[b, i, :, part(r, b)],
+                ("second", b, g and 1), passed[r].at[b, i, :, part(r, b)],
                 second[r].at[b, i, :, part(r, b)], outer=neighbour[other],
             )
 
@@ -224,9 +228,11 @@
         return total + up(second[r][b, i, :, at])
 
     def send_third(b):
-        groups = others_of if late(b) else tail
-        for g in groups:
-            arrive(("second", b, g), deltas.at[b, at_rows(g), :, pl.ds(0, pair_width(b))])
+        width = pl.ds(0, pair_width(b))
+        if late(b):
+            arrive(("second", b, 1), deltas.at[b, pl.ds(0, rep_count - 1), :, width])
+        else:
+            arrive(("second", b, None), deltas.at[b, :, :, width])
         for d in others_of:
             there = (q + d) % rep_count
             for r in range(2):
@@ -525,27 +531,20 @@
         def deep_rows(count):
             return deltas.at[pl.ds(0, some), pl.ds(0, count), :, pl.ds(0, pod_count * deeps // some)]
 
-        leave("first", deltas.at[pl.ds(0, SIDE), :, :, pl.ds(0, pairs)])
-        leave("second", rows(rep_count, pairs))
+        leave("first", deltas.at[pl.ds(0, SIDE + 1), :, :, pl.ds(0, pairs)])
         leave("third", rows(rep_count - 1, pairs))
         leave("near", deep_rows(3))
-        leave("far", deep_rows(2))
-        leave("last", deep_rows(1))
+        leave("far", deep_rows(3))
         leave("cross", rows(pod_count - 1, deeps))
-        leave("early", arecv.at[pl.ds(1, pod_count - 1)])
+        leave("early", deltas.at[pl.ds(0, pod_count - 1), pl.ds(0, SIDE * slots), :, pl.ds(0, arecv.shape[3])])
         leave("norm", others.at[pl.ds(0, group * shard_count - 1)])
-        leave("slot", slotted.at[pl.ds(1, pod_count - 1)])
         leave("shard", others.at[pl.ds(0, 1)])
         leave("wide", out.at[:, 0, :, pl.ds(0, wc)])
         leave("wider", out.at[:, 0, :, pl.ds(0, SIDE * wc)])
-        leave("up", out.at[:, 0, :, pl.ds(0, wa + wb)])
-        leave("over", out.at[:, pl.ds(0, 2), :, pl.ds(0, wa + wb)])
-        leave("down", out.at[:, pl.ds(0, 3), :, pl.ds(0, wa + wb)])
-        leave("outward", out.at[:, 0, :, whole])
-        leave("across", out.at[:, pl.ds(0, 2), :, whole])
-        leave("inward", out.at[:, pl.ds(0, 3), :, whole])
-        leave("block", out.at[:, :, :, pl.ds(0, wa + wb)])
-        leave("blocks", out.at[:, :, :, pl.ds(0, SIDE * (wa + wb))])
+        leave("up", out.at[:, 0, :, pl.ds(0, wa + wb + pod_count * wc)])
+        leave("over", out.at[:, pl.ds(0, 2), :, pl.ds(0, wa + wb + pod_count * wc)])
+        leave("down", out.at[:, pl.ds(0, 3), :, pl.ds(0, wa + wb + pod_count * wc)])
+        leave("block", out.at[:, :, :, pl.ds(0, (1 + SIDE) * (wa + wb))])
 
     def rests(b):
         pl.when(is_tip)(lambda: arrive(("down", b), line_rows(b, 3)))
@@ -702,7 +701,7 @@
     part, deep_width = width // pod_count, extra + wc
     deep = pod_count * deep_width
     group = pod_count * rep_count
-    reduce_waits = 2 * (blocks + (rep_count - 1) * LATE) + 8 * blocks
+    reduce_waits = 2 * blocks + rep_count * LATE + 8 * blocks
     waits = 5 + max(reduce_waits, blocks * (rep_count + 9) + 2)
     vmem, hbm = pl.BlockSpec(memory_space=pltpu.VMEM), pl.BlockSpec(memory_space=pltpu.HBM)
     bf16, f32 = jnp.bfloat16, jnp.float32

time: 96.9 us -> 96.8 us (level)
  no operation moved by 1% of the time
where the time goes in v7:
time: 96.8 us; the launch traced here: 96.6 us
  Pallas kernels  96 us (99%)
    pallas_call x1, Pallas kernels, fused(): pl.pallas_call(functools.partial(kernel, widths, (pod_count, rep_count, s...  92.8 us
    pallas_call x1, Pallas kernels, fused(): pl.pallas_call(store, out_shape=tuple((jax.ShapeDtypeStruct(a.shape, a.dt...  3.23 us

profile of v7, /device:TPU:0, one launch (start us, length us, event | category | flops | bytes accessed | tf_op | source)
XLA Modules:
  0.0 96.6 jit_solution(7840803161325299844)
XLA Ops:
  0.6 92.8 %shard_map.67 = (bf16[4,4,32,5120]{3,2,1,0:T(8,128)(2,1)S(1)}, f32[2,32,5120]{2,1,0:T(8,128)S(1)}, f32[2,32,5120]{2,1,0:T(8,128)S(1)}) custom-call(s32[4]{0:T(128)} %bitcast.10, bf16[4,4,32,5120]{3,2,1,0:T(8,128)(2,1)} %bitcast.7, f32[2,32,5120]{2,1,0:T(8,128)} %bitcast.8, f32[2,32,5120]{2,1,0:T(8,128)} %bitcast.9), custom_call_target="tpu_custom_call" | custom-call | tf_op jit(solution)/shard_map/pallas_call | solution.py:709
  93.4 3.2 %shard_map.68 = (bf16[4,4,32,5120]{3,2,1,0:T(8,128)(2,1)}, f32[2,32,5120]{2,1,0:T(8,128)}, f32[2,32,5120]{2,1,0:T(8,128)}) custom-call(bf16[4,4,32,5120]{3,2,1,0:T(8,128)(2,1)S(1)} %get-tuple-element.9.refs_0_, f32[2,32,5120]{2,1,0:T(8,128)S(1)} %get-tuple-element.10.refs_1_, f32[2,32,5120]{2,1,0:T(8,128)S(1)} %get-tuple-element.11.refs_2_), custom_call_target="tpu_custom_call" | custom-call | tf_op jit(solution)/shard_map/pallas_call | solution.py:757
